TPU v7x, 32 devices: a whole 2x2x4 slice. The times are simulated.
32 devices in a mesh: layer: 8 (over y, x, core), tensor: 4 (over z).
Axes of the slice: x: 2, y: 2, z: 4, core: 2. Of those that a mesh axis runs over, the one named last changes fastest.
Arguments:
- gradient: bfloat16 [8, 1024, 8192], P(None, 'tensor', 'layer'), may hold values from -8 to 8
- row_basis: bfloat16 [8, 1024, 256], P('layer', 'tensor'), may hold values from -0.1875 to 0.1875
- column_basis: bfloat16 [8, 8192, 256], P('layer', 'tensor'), may hold values from -0.0625 to 0.0625
- row_eigen: float32 [8, 256], P('layer'), may hold values from 0.01 to 10
- column_eigen: float32 [8, 256], P('layer'), may hold values from 0.01 to 10
- row_escape: float32 [8], P('layer'), may hold values from 0.02 to 0.2
- column_escape: float32 [8], P('layer'), may hold values from 0.02 to 0.2
Outputs:
- update: bfloat16 [8, 1024, 8192], P(None, 'tensor', 'layer')
All inputs are finite; a program needn't handle non-finite values.
Results may differ from a plain program's by a relative error of at most 0.0055.
Values may be sent and summed in bfloat16 or wider, within the bound.
A program may use at most 128 MiB of HBM per device.

v0:
```python
import functools

import jax
import jax.numpy as jnp
from jax import lax
from jax.experimental import pallas as pl
from jax.experimental.pallas import tpu as pltpu
from jax.sharding import PartitionSpec as P

MESH = pl.DeviceIdType.MESH
F32 = jnp.float32
BF16 = jnp.bfloat16


def remote(src, dst, send, recv, axis, index):
    return pltpu.make_async_remote_copy(
        src_ref=src,
        dst_ref=dst,
        send_sem=send,
        recv_sem=recv,
        device_id={axis: index},
        device_id_type=MESH,
    )


def loop(lo, hi, fn):
    def step(i, carry):
        fn(i)
        return carry

    lax.fori_loop(lo, hi, step, 0)


def dot(a, b):
    return jnp.dot(a, b, preferred_element_type=F32)


def kernel(
    L, T,
    g, rows_basis, rows_basis_t, cols, dr, dc, base,
    out, factor,
    gg, own, pin, qin, pout, qout, call, mid, left, core_out, core_in, core_sum, raw_out,
    gacc, uacc, nsend, nrecv, fsend, frecv,
    gs, gr, cs, cr, ps, pr, qs, qr, ks, kr, os_, or_, ns, nr, fs, fr,
):
    me = lax.axis_index("layer")
    t = lax.axis_index("tensor")
    W = g.shape[2]
    Cr = cols.shape[0]
    right, lft = t + 1, t - 1
    has_right, has_left = t < T - 1, t > 0

    barrier = pltpu.get_barrier_semaphore()
    loop(1, L, lambda d: pl.semaphore_signal(
        barrier, inc=1, device_id={"layer": lax.rem(me + d, L)}, device_id_type=MESH))
    loop(1, T, lambda d: pl.semaphore_signal(
        barrier, inc=1, device_id={"tensor": lax.rem(t + d, T)}, device_id_type=MESH))
    pl.semaphore_wait(barrier, L + T - 2)

    def g_copy(slot, dst):
        return remote(g.at[dst], gg.at[slot], gs.at[dst], gr.at[slot], "layer", dst)

    def c_rows(s):
        return call.at[pl.ds(pl.multiple_of(s * Cr, Cr), Cr)]

    def c_copy(src, s, h, side):
        return remote(src, c_rows(s), cs.at[side, h], cr.at[s], "tensor", right if side == 0 else lft)

    pl.when(has_right)(lambda: c_copy(cols, t, 0, 0).start())
    pl.when(has_left)(lambda: c_copy(cols, t, 0, 1).start())
    loop(1, L, lambda d: g_copy(me, lax.rem(me + d, L)).start())
    gg[me] = g[me]
    call[pl.ds(pl.multiple_of(t * Cr, Cr), Cr), :] = cols[...]
    gacc[...] = jnp.zeros_like(gacc)
    uacc[...] = jnp.zeros_like(uacc)
    mid[...] = jnp.zeros_like(mid)

    @pl.when(t == 0)
    def _():
        loop(0, L, lambda d: pin.__setitem__(d, jnp.zeros(pin.shape[1:], BF16)))

    @pl.when(t == T - 1)
    def _():
        loop(0, L, lambda d: qin.__setitem__(d, jnp.zeros(qin.shape[1:], BF16)))

    def c_hop(h):
        @pl.when(t - h >= 0)
        def _():
            c_copy(cols, t - h, 0, 0).wait_recv()
            pl.when(has_right)(lambda: c_copy(c_rows(t - h), t - h, h, 0).start())

        @pl.when(t + h < T)
        def _():
            c_copy(cols, t + h, 0, 1).wait_recv()
            pl.when(has_left)(lambda: c_copy(c_rows(t + h), t + h, h, 1).start())

    def p_copy(src, d):
        return remote(src, pin.at[d], ps.at[d], pr.at[d], "tensor", right)

    def q_copy(src, d):
        return remote(src, qin.at[d], qs.at[d], qr.at[d], "tensor", lft)

    def end_send(d):
        pl.when(t == 0)(lambda: p_copy(own.at[d], d).start())
        pl.when(t == T - 1)(lambda: q_copy(own.at[d], d).start())

    def forward(k):
        d = k - t

        @pl.when((d >= 0) & (d < L) & has_left)
        def _():
            p_copy(own.at[d], d).wait_recv()

            @pl.when(has_right)
            def _():
                pout[d] = (pin[d].astype(F32) + own[d].astype(F32)).astype(BF16)
                p_copy(pout.at[d], d).start()

        e = k - (T - 1 - t)

        @pl.when((e >= 0) & (e < L) & has_right)
        def _():
            q_copy(own.at[e], e).wait_recv()

            @pl.when(has_left)
            def _():
                qout[e] = (qin[e].astype(F32) + own[e].astype(F32)).astype(BF16)
                q_copy(qout.at[e], e).start()

    half = L // 2
    early = ((T - 2) * L) // (T - 1) + 1

    def arrive(d):
        j = lax.rem(me - 1 - d + L, L)
        pl.when(d < L - 1)(lambda: g_copy(j, j).wait_recv())
        block = gg[j]
        own[d] = dot(rows_basis_t[...], block).astype(BF16)
        pl.when(d <= half)(lambda: end_send(d))
        wide = block.astype(F32)
        gacc[...] += jnp.sum(wide * wide, axis=0, keepdims=True)
        for h in range(1, T - 1):
            pl.when(d == (h * L) // (T - 1))(lambda h=h: c_hop(h))
        pl.when(d >= early)(lambda: forward(d - early + 1))

    loop(0, L, arrive)
    c_hop(T - 1)

    def mid_step(j):
        mid[...] += dot(gg[j], call[pl.ds(pl.multiple_of(j * W, W), W), :])

    loop(0, L, mid_step)
    core_out[...] = dot(rows_basis_t[...], mid[...].astype(BF16)).astype(BF16)

    def kp_copy(src):
        return remote(src, core_in.at[0], ks.at[0], kr.at[0], "tensor", right)

    def kq_copy(src):
        return remote(src, core_in.at[1], ks.at[1], kr.at[1], "tensor", lft)

    @pl.when(t == 0)
    def _():
        core_in[0] = jnp.zeros(core_out.shape, BF16)
        kp_copy(core_out).start()

    @pl.when(t == T - 1)
    def _():
        core_in[1] = jnp.zeros(core_out.shape, BF16)
        kq_copy(core_out).start()

    loop(half + 1, L, end_send)

    def core_step(k):
        @pl.when((k == half + t) & has_left)
        def _():
            kp_copy(core_out).wait_recv()

            @pl.when(has_right)
            def _():
                core_sum[0] = (core_in[0].astype(F32) + core_out[...].astype(F32)).astype(BF16)
                kp_copy(core_sum.at[0]).start()

        @pl.when((k == half + T - 1 - t) & has_right)
        def _():
            kq_copy(core_out).wait_recv()

            @pl.when(has_left)
            def _():
                core_sum[1] = (core_in[1].astype(F32) + core_out[...].astype(F32)).astype(BF16)
                kq_copy(core_sum.at[1]).start()

    def make_left():
        core = core_in[0].astype(F32) + core_in[1].astype(F32) + core_out[...].astype(F32)
        core = (core * dr[:, :1]).astype(BF16)
        mixed = base[0:1, 0:1] * mid[...] + dot(rows_basis[...], core)
        left[...] = (mixed * dc[0:1, :]).astype(BF16)

    def o_copy(slot, dst):
        return remote(raw_out.at[dst], out.at[slot], os_.at[dst], or_.at[slot], "layer", dst)

    def own_copy():
        return pltpu.make_async_copy(raw_out.at[me], out.at[me], os_.at[me])

    def emit(d):
        j = lax.rem(me - 1 - d + L, L)
        total = own[d].astype(F32) + pin[d].astype(F32) + qin[d].astype(F32)
        scaled = (total * dr[:, :1]).astype(BF16)
        raw = base[2:3, 0:1] * gg[j].astype(F32)
        raw = raw + base[1:2, 0:1] * dot(rows_basis[...], scaled)
        raw = raw + lax.dot_general(
            left[...], call[pl.ds(pl.multiple_of(j * W, W), W), :],
            (((1,), (1,)), ((), ())), preferred_element_type=F32)
        raw_out[j] = raw.astype(BF16)
        pl.when(d == L - 1)(lambda: own_copy().start())
        pl.when(d < L - 1)(lambda: o_copy(me, j).start())
        uacc[...] += jnp.sum(raw * raw, axis=0, keepdims=True)

    first = half + T - 1

    def upto(k):
        paced = jnp.minimum(k - T + 2, 3 + 2 * (k - first))
        return jnp.where(has_left & has_right, paced, k - T + 2)

    def tail_step(k):
        core_step(k)
        forward(k)
        pl.when(k == first)(make_left)
        pl.when(k == first)(lambda: loop(0, upto(k), emit))
        pl.when(k > first)(lambda: loop(upto(k - 1), upto(k), emit))

    loop(L - early + 1, L + T - 1, tail_step)

    nsend[0:8, :] = jnp.broadcast_to(jnp.sum(gacc[...]), (8, 128))
    nsend[8:16, :] = jnp.broadcast_to(jnp.sum(uacc[...]), (8, 128))

    def n_copy(slot, dst):
        return remote(nsend, nrecv.at[slot], ns.at[dst], nr.at[slot], "tensor", dst)

    loop(1, T, lambda d: n_copy(t, lax.rem(t + d, T)).start())
    nrecv[t] = nsend[...]
    for d in range(1, T):
        s = lax.rem(t + d, T)
        n_copy(s, s).wait_recv()
    sq = nrecv[0]
    for s in range(1, T):
        sq = sq + nrecv[s]
    fsend[...] = jnp.sqrt((sq[0:8] + 1.0) / (sq[8:16] + 1.0))

    def f_copy(slot, dst):
        return remote(fsend, frecv.at[slot], fs.at[dst], fr.at[slot], "layer", dst)

    loop(1, L, lambda d: f_copy(me, lax.rem(me + d, L)).start())
    frecv[me] = fsend[...]
    own_copy().wait()

    def finish(d):
        j = lax.rem(me + d, L)
        o_copy(j, j).wait_recv()
        f_copy(j, j).wait_recv()

    loop(1, L, finish)
    factor[...] = frecv[...]

    def drain_layer(d):
        j = lax.rem(me + d, L)
        g_copy(me, j).wait_send()
        o_copy(me, j).wait_send()
        f_copy(me, j).wait_send()

    loop(1, L, drain_layer)
    pl.when(has_right)(lambda: kp_copy(core_out).wait_send())
    pl.when(has_left)(lambda: kq_copy(core_out).wait_send())

    def drain_tensor(d):
        s = lax.rem(t + d, T)
        n_copy(t, s).wait_send()

    loop(1, T, drain_tensor)

    def drain_line(d):
        pl.when(has_right)(lambda: p_copy(own.at[d], d).wait_send())
        pl.when(has_left)(lambda: q_copy(own.at[d], d).wait_send())

    loop(0, L, drain_line)
    for h in range(T - 1):
        pl.when((t - h >= 0) & has_right)(lambda h=h: c_copy(cols, t, h, 0).wait_send())
        pl.when((t + h < T) & has_left)(lambda h=h: c_copy(cols, t, h, 1).wait_send())


def solution(mesh):
    L, T = mesh.shape["layer"], mesh.shape["tensor"]

    def body(gradient, row_basis, column_basis, row_eigen, column_eigen, row_escape, column_escape):
        row_base = row_escape ** (-0.25)
        column_base = column_escape ** (-0.25)
        row_coef = (row_eigen + row_escape[:, None]) ** (-0.25) - row_base[:, None]
        column_coef = (column_eigen + column_escape[:, None]) ** (-0.25) - column_base[:, None]
        _, r, W = gradient.shape
        _, Cr, K = column_basis.shape
        dr = jnp.broadcast_to(row_coef[0][:, None], (K, 128))
        dc = jnp.broadcast_to(column_coef, (8, K))
        base = jnp.broadcast_to(
            jnp.concatenate([row_base, column_base, row_base * column_base] + [row_base] * 5)[:, None], (8, 128))
        vmem = pl.BlockSpec(memory_space=pltpu.VMEM)
        chunk = pltpu.VMEM((L, K, W), BF16)
        block = pltpu.VMEM((L, r, W), BF16)
        sem = pltpu.SemaphoreType.DMA
        raw, factor = pl.pallas_call(
            functools.partial(kernel, L, T),
            out_shape=(jax.ShapeDtypeStruct((L, r, W), BF16), jax.ShapeDtypeStruct((L, 8, 128), F32)),
            in_specs=[vmem] * 7,
            out_specs=(pl.BlockSpec(memory_space=pl.ANY), vmem),
            scratch_shapes=[
                block, chunk, chunk, chunk, chunk, chunk,
                pltpu.VMEM((T * Cr, K), BF16),
                pltpu.VMEM((r, K), F32),
                pltpu.VMEM((r, K), BF16),
                pltpu.VMEM((K, K), BF16),
                pltpu.VMEM((2, K, K), BF16),
                pltpu.VMEM((2, K, K), BF16),
                block,
                pltpu.VMEM((1, W), F32),
                pltpu.VMEM((1, W), F32),
                pltpu.VMEM((16, 128), F32),
                pltpu.VMEM((T, 16, 128), F32),
                pltpu.VMEM((8, 128), F32),
                pltpu.VMEM((L, 8, 128), F32),
                sem((L,)), sem((L,)),
                sem((2, T)), sem((T,)),
                sem((L,)), sem((L,)),
                sem((L,)), sem((L,)),
                sem((2,)), sem((2,)),
                sem((L,)), sem((L,)),
                sem((T,)), sem((T,)),
                sem((L,)), sem((L,)),
            ],
            compiler_params=pltpu.CompilerParams(
                collective_id=0, has_side_effects=True, vmem_limit_bytes=62 * 1024 * 1024),
        )(gradient, row_basis[0], row_basis[0].T, column_basis[0], dr, dc, base)
        return (raw.astype(F32) * factor[:, :1, :1]).astype(BF16)

    in_specs = (
        P(None, "tensor", "layer"),
        P("layer", "tensor", None),
        P("layer", "tensor", None),
        P("layer", None),
        P("layer", None),
        P("layer"),
        P("layer"),
    )
    out_specs = P(None, "tensor", "layer")
    return jax.shard_map(body, mesh=mesh, in_specs=in_specs, out_specs=out_specs, check_vma=False)
```

profile of v0, /device:TPU:0, one launch (start us, length us, event | category | flops | bytes accessed | tf_op | source)
XLA Modules:
  0.0 203.8 jit_solution(12756830800866886340)
XLA Ops:
  1.4 0.1 concatenate.3
  1.5 0.7 power_subtract_fusion
  2.2 0.7 power_subtract_fusion.1
  2.9 0.7 broadcast_in_dim.28.base
  3.5 0.6 broadcast_in_dim.13.dc
  4.1 0.7 broadcast_in_dim.11.dr
  4.9 1.7 copy.10
  6.5 190.4 %shard_map.73 = (bf16[8,256,1024]{2,1,0:T(8,128)(2,1)}, f32[8,8,128]{2,1,0:T(8,128)}) custom-call(bf16[8,256,1024]{2,1,0:T(8,128)(2,1)} %g.1, bf16[256,256]{1,0:T(8,128)(2,1)} %bitcast.14, bf16[256,256]{1,0:T(8,128)(2,1)} %bitcast.15, bf16[2048,256]{1,0:T(8,128)(2,1)} %bitcast.13, f32[256,128]{1,0:T(8,128)} %broadcast_in_dim.11.dr, ...), custom_call_target="tpu_custom_call" | custom-call | tf_op jit(solution)/shard_map/pallas_call | solution.py:307
  196.9 0.9 slice_reduce_fusion
  197.8 6.0 %multiply_convert_fusion = bf16[8,256,1024]{2,1,0:T(8,128)(2,1)} fusion(bf16[8,256,1024]{2,1,0:T(8,128)(2,1)} %get-tuple-element.7, f32[8]{0:T(128)S(1)} %slice_reduce_fusion), kind=kLoop, calls=%fused_computation | loop fusion | flops 6291456 | bytes 8388640 | tf_op jit(solution)/shard_map/convert_element_type | solution.py:339
where the time goes:
time: 204 us
  Pallas kernels  190 us (93%)
  other arithmetic  7.37 us (4%)
  local copies, waits for them, and re-layouts  4.65 us (2%)
    pallas_call x1, Pallas kernels, body(): pl.pallas_call(functools.partial(kernel, L, T), out_shape=(jax.ShapeDtype...  190 us
    convert_element_type x1, other arithmetic, body(): return (raw.astype(F32) * factor[:, :1, :1]).astype(BF16)  5.97 us

commit v1 on v0

v1 whole, which is shorter than its diff:
```python
import functools

import jax
import jax.numpy as jnp
from jax import lax
from jax.experimental import pallas as pl
from jax.experimental.pallas import tpu as pltpu
from jax.sharding import PartitionSpec as P

MESH = pl.DeviceIdType.MESH
F32 = jnp.float32
BF16 = jnp.bfloat16


def remote(src, dst, send, recv, axis, index):
    return pltpu.make_async_remote_copy(
        src_ref=src,
        dst_ref=dst,
        send_sem=send,
        recv_sem=recv,
        device_id={axis: index},
        device_id_type=MESH,
    )


def loop(lo, hi, fn):
    def step(i, carry):
        fn(i)
        return carry

    lax.fori_loop(lo, hi, step, 0)


def dot(a, b, dims=((1,), (0,))):
    return lax.dot_general(a, b, (dims, ((), ())), preferred_element_type=F32)


def quarter(x):
    return lax.rsqrt(jnp.sqrt(x))


def lanes(x):
    s = jnp.sum(x * x, axis=0, keepdims=True)
    out = s[:, 0:128]
    for k in range(1, x.shape[1] // 128):
        out = out + s[:, k * 128:(k + 1) * 128]
    return out


def kernel(
    L, T, NP,
    g, u, cols, reig, ceig, resc, cesc,
    raw, factor,
    uall, vall, vline, own, pin, qin, mout, mi, mid, lall, core_in, cb,
    nsend, tile, nin, fsend, fin,
    us, ur, bs, br, vs, vr, xs, xr, ms, mr, ks, kr, ls, lr, ps, pr, qs, qr, ns, nr, fs, fr,
):
    me = lax.axis_index("layer")
    t = lax.axis_index("tensor")
    W = g.shape[2]
    Cr = cols.shape[0]
    B = Cr // W
    BP = B // NP
    PR = Cr // NP
    K = u.shape[1]
    right, lft = t + 1, t - 1
    has_right, has_left = t < T - 1, t > 0
    inner = has_right & has_left
    far = jnp.maximum(t, T - 1 - t)

    barrier = pltpu.get_barrier_semaphore()
    loop(1, L, lambda d: pl.semaphore_signal(
        barrier, inc=1, device_id={"layer": lax.rem(me + d, L)}, device_id_type=MESH))
    loop(1, T, lambda d: pl.semaphore_signal(
        barrier, inc=1, device_id={"tensor": lax.rem(t + d, T)}, device_id_type=MESH))

    row_base = quarter(resc[...])
    column_base = quarter(cesc[...])
    row_coef = quarter(reig[...] + resc[...]) - row_base
    dc = quarter(ceig[...] + cesc[...]) - column_base
    cb[me, 0:1, :] = row_coef * column_base
    cb[me, 1:2, :] = jnp.broadcast_to(row_base * column_base, (1, K))
    cb[me, 2:8, :] = jnp.broadcast_to(row_coef, (6, K))
    uall[me] = u[...]

    pl.semaphore_wait(barrier, L + T - 2)

    def layer_of(d):
        return lax.rem(me - d + L, L)

    def v_copy(src, c, i, side):
        return remote(src, vline.at[c, i], vs.at[side, c, i], vr.at[c, i], "tensor",
                      right if side == 0 else lft)

    def x_copy(src, slot, dst):
        return remote(src, vall.at[slot], xs.at[dst], xr.at[slot], "layer", dst)

    def u_copy(slot, dst):
        return remote(u, uall.at[slot], us.at[dst], ur.at[slot], "layer", dst)

    def b_copy(slot, dst):
        return remote(cb.at[me], cb.at[slot], bs.at[dst], br.at[slot], "layer", dst)

    def m_copy(slot, dst):
        return remote(mout.at[dst], mi.at[slot], ms.at[dst], mr.at[slot], "layer", dst)

    def l_copy(slot, dst):
        return remote(lall.at[me], lall.at[slot], ls.at[dst], lr.at[slot], "layer", dst)

    def k_copy(slot, dst):
        return remote(core_in.at[t], core_in.at[slot], ks.at[dst], kr.at[slot], "tensor", dst)

    def p_copy(src, d):
        return remote(src, pin.at[d], ps.at[d], pr.at[d], "tensor", right)

    def q_copy(src, d):
        return remote(src, qin.at[d], qs.at[d], qr.at[d], "tensor", lft)

    def piece(i):
        return cols.at[pl.ds(i * PR, PR)]

    for i in range(NP):
        pl.when(has_right)(lambda i=i: v_copy(piece(i), t, i, 0).start())
        pl.when(has_left)(lambda i=i: v_copy(piece(i), t, i, 1).start())

    def send_basis(d):
        dst = lax.rem(me + d, L)
        u_copy(me, dst).start()
        b_copy(me, dst).start()

    loop(1, L, send_basis)

    def spread(c, i, rows):
        def one(b):
            dst = c * B + i * BP + b
            pl.when(dst != me)(lambda: x_copy(rows(b), me, dst).start())

            @pl.when(dst == me)
            def _():
                vall[me] = rows(b)[...]

        loop(0, BP, one)

    for i in range(NP):
        spread(t, i, lambda b, i=i: cols.at[pl.ds(pl.multiple_of(i * PR + b * W, 128), W)])

    @pl.when(t == 0)
    def _():
        loop(0, L, lambda d: pin.__setitem__(d, jnp.zeros(pin.shape[1:], BF16)))

    @pl.when(t == T - 1)
    def _():
        loop(0, L, lambda d: qin.__setitem__(d, jnp.zeros(qin.shape[1:], BF16)))

    def project(d):
        l = layer_of(d)

        @pl.when(d > 0)
        def _():
            u_copy(l, l).wait_recv()
            b_copy(l, l).wait_recv()

        block = g[l]
        own[d] = dot(uall[l], block, ((0,), (0,))).astype(BF16)
        nsend[0, pl.ds(l, 1), :] = lanes(block.astype(F32))

    loop(0, L, project)

    def end_send(d):
        @pl.when((d >= 0) & (d < L))
        def _():
            pl.when(t == 0)(lambda: p_copy(own.at[d], d).start())
            pl.when(t == T - 1)(lambda: q_copy(own.at[d], d).start())

    def forward_p(d):
        @pl.when((d >= 0) & (d < L) & has_left)
        def _():
            p_copy(own.at[d], d).wait_recv()

            @pl.when(has_right)
            def _():
                pin[d] = (pin[d].astype(F32) + own[d].astype(F32)).astype(BF16)
                p_copy(pin.at[d], d).start()

    def forward_q(d):
        @pl.when((d >= 0) & (d < L) & has_right)
        def _():
            q_copy(own.at[d], d).wait_recv()

            @pl.when(has_left)
            def _():
                qin[d] = (qin[d].astype(F32) + own[d].astype(F32)).astype(BF16)
                q_copy(qin.at[d], d).start()

    def relay(h, i):
        for side, c, ok, onward in ((0, t - h, t - h >= 0, has_right), (1, t + h, t + h < T, has_left)):
            @pl.when(ok)
            def _(side=side, c=c, onward=onward):
                v_copy(vline.at[c, i], c, i, side).wait_recv()
                pl.when(onward)(lambda: v_copy(vline.at[c, i], c, i, side).start())
                spread(c, i, lambda b: vline.at[c, i, pl.ds(pl.multiple_of(b * W, 128), W)])

    def middle(d):
        l = layer_of(d)
        pl.when(d > 0)(lambda: x_copy(vall.at[l], l, l).wait_recv())
        m = dot(g[l], vall[l]).astype(BF16)

        @pl.when(d == 0)
        def _():
            mi[me] = m

        @pl.when(d > 0)
        def _():
            mout[l] = m
            m_copy(me, l).start()

    def gather_middle():
        total = mi[me].astype(F32)
        mid[...] = total

        def add(d):
            l = layer_of(d)
            m_copy(l, l).wait_recv()
            mid[...] += mi[l].astype(F32)

        loop(1, L, add)
        core_in[t] = dot(u[...], mid[...].astype(BF16), ((0,), (0,))).astype(BF16)
        loop(1, T, lambda d: k_copy(t, lax.rem(t + d, T)).start())

    def make_left():
        def wait(d):
            s = lax.rem(t + d, T)
            k_copy(s, s).wait_recv()

        loop(1, T, wait)
        core = core_in[0].astype(F32)
        for s in range(1, T):
            core = core + core_in[s].astype(F32)
        core = (core * jnp.transpose(cb[me])[:, 2:3]).astype(BF16)
        mixed = row_base * mid[...] + dot(u[...], core)
        lall[me] = (mixed * dc).astype(BF16)
        loop(1, L, lambda d: l_copy(me, lax.rem(me + d, L)).start())

    sign = jnp.where(inner, -1.0, 1.0).astype(F32)

    def emit(d):
        l = layer_of(d)
        pl.when(d > 0)(lambda: l_copy(l, l).wait_recv())
        total = pin[d].astype(F32) + qin[d].astype(F32) + sign * own[d].astype(F32)
        scaled = (total * jnp.transpose(cb[l])[:, 0:1]).astype(BF16)
        x = cb[l, 1:2, 0:1] * g[l].astype(F32)
        x = x + dot(uall[l], scaled)
        x = x + dot(lall[l], vall[l], ((1,), (1,)))
        raw[l] = x.astype(BF16)
        nsend[1, pl.ds(l, 1), :] = lanes(x)

    blk = lax.div(lax.rem(me, B), BP)
    dist = jnp.abs(t - lax.div(me, B))
    first = jnp.where(dist == 0, 1, NP * (dist - 1) + blk + 1)
    per = max(L // 4, 1)
    at_core = NP * far + 4
    at_left = NP * (T - 1) + 5
    last = max(NP * (T - 1) + L, at_left + 1)

    def emitted(s):
        return jnp.where(s > at_left, jnp.clip(s - NP * far, 0, L), 0)

    def step(s):
        pl.when(s <= NP * (T - 1))(
            lambda: relay(lax.div(s - 1, NP) + 1, lax.rem(s - 1, NP)))
        end_send(s - 1)
        forward_p(s - NP * t - 1)
        forward_q(s - NP * (T - 1 - t) - 1)
        loop(jnp.clip(per * (s - first - 1), 0, L), jnp.clip(per * (s - first), 0, L), middle)
        pl.when(s == at_core)(gather_middle)
        pl.when(s == at_left)(make_left)
        loop(emitted(s - 1), emitted(s), emit)

    loop(1, last + 1, step)

    tile[...] = jnp.zeros_like(tile)
    tile[0:2, 0:L] = jnp.sum(nsend[...], axis=2)

    def n_copy(slot, dst):
        return remote(tile, nin.at[slot], ns.at[dst], nr.at[slot], "tensor", dst)

    loop(1, T, lambda d: n_copy(t, lax.rem(t + d, T)).start())
    nin[t] = tile[...]
    for d in range(1, T):
        s = lax.rem(t + d, T)
        n_copy(s, s).wait_recv()
    sq = nin[0]
    for s in range(1, T):
        sq = sq + nin[s]
    fsend[...] = sq

    def f_copy(slot, dst):
        return remote(fsend, fin.at[slot], fs.at[dst], fr.at[slot], "layer", dst)

    loop(1, L, lambda d: f_copy(me, lax.rem(me + d, L)).start())
    fin[me] = sq

    def finish(d):
        j = lax.rem(me + d, L)
        f_copy(j, j).wait_recv()

    loop(1, L, finish)
    tot = jnp.sum(fin[...], axis=0)
    factor[...] = jnp.broadcast_to(jnp.sqrt((tot[0:1] + 1.0) / (tot[1:2] + 1.0)), factor.shape)

    def drain_layer(d):
        j = lax.rem(me + d, L)
        u_copy(me, j).wait_send()
        b_copy(me, j).wait_send()
        x_copy(vall.at[me], me, j).wait_send()
        m_copy(me, j).wait_send()
        l_copy(me, j).wait_send()
        f_copy(me, j).wait_send()

    loop(1, L, drain_layer)

    def drain_tensor(d):
        s = lax.rem(t + d, T)
        k_copy(t, s).wait_send()
        n_copy(t, s).wait_send()

    loop(1, T, drain_tensor)

    def drain_line(d):
        pl.when(has_right)(lambda: p_copy(own.at[d], d).wait_send())
        pl.when(has_left)(lambda: q_copy(own.at[d], d).wait_send())

    loop(0, L, drain_line)

    def drain_v(c):
        for i in range(NP):
            pl.when((c <= t) & has_right)(lambda i=i: v_copy(piece(i), c, i, 0).wait_send())
            pl.when((c >= t) & has_left)(lambda i=i: v_copy(piece(i), c, i, 1).wait_send())

    loop(0, T, drain_v)


def solution(mesh):
    L, T = mesh.shape["layer"], mesh.shape["tensor"]
    NP = 2

    def body(gradient, row_basis, column_basis, row_eigen, column_eigen, row_escape, column_escape):
        _, r, W = gradient.shape
        _, Cr, K = column_basis.shape
        vmem = pl.BlockSpec(memory_space=pltpu.VMEM)
        chunk = pltpu.VMEM((L, K, W), BF16)
        small = pltpu.VMEM((L, r, K), BF16)
        sem = pltpu.SemaphoreType.DMA
        norms = pltpu.VMEM((8, 128), F32)
        raw, factor = pl.pallas_call(
            functools.partial(kernel, L, T, NP),
            out_shape=(jax.ShapeDtypeStruct((L, r, W), BF16), jax.ShapeDtypeStruct((8, 128), F32)),
            in_specs=[vmem] * 7,
            out_specs=(vmem, vmem),
            scratch_shapes=[
                small,
                pltpu.VMEM((L, W, K), BF16),
                pltpu.VMEM((T, NP, Cr // NP, K), BF16),
                chunk, chunk, chunk,
                small, small,
                pltpu.VMEM((r, K), F32),
                small,
                pltpu.VMEM((T, K, K), BF16),
                pltpu.VMEM((L, 8, K), F32),
                pltpu.VMEM((2, L, 128), F32),
                norms, pltpu.VMEM((T, 8, 128), F32),
                norms, pltpu.VMEM((L, 8, 128), F32),
                sem((L,)), sem((L,)),
                sem((L,)), sem((L,)),
                sem((2, T, NP)), sem((T, NP)),
                sem((L,)), sem((L,)),
                sem((L,)), sem((L,)),
                sem((T,)), sem((T,)),
                sem((L,)), sem((L,)),
                sem((L,)), sem((L,)),
                sem((L,)), sem((L,)),
                sem((T,)), sem((T,)),
                sem((L,)), sem((L,)),
            ],
            compiler_params=pltpu.CompilerParams(
                collective_id=0, has_side_effects=True, vmem_limit_bytes=63 * 1024 * 1024),
        )(gradient, row_basis[0], column_basis[0], row_eigen, column_eigen,
          row_escape[:, None], column_escape[:, None])
        return (raw.astype(F32) * factor[0, :L, None, None]).astype(BF16)

    in_specs = (
        P(None, "tensor", "layer"),
        P("layer", "tensor", None),
        P("layer", "tensor", None),
        P("layer", None),
        P("layer", None),
        P("layer"),
        P("layer"),
    )
    out_specs = P(None, "tensor", "layer")
    return jax.shard_map(body, mesh=mesh, in_specs=in_specs, out_specs=out_specs, check_vma=False)
```

time: 204 us -> 194 us (0.951)
  Pallas kernels: 190 us -> 186 us
  local copies, waits for them, and re-layouts: 4.65 us -> 0.68 us
    pallas_call x1, Pallas kernels: 190 us -> 186 us  [body(): pl.pallas_call(functools.partial(kernel, L, T, NP), out_shape=(jax.ShapeD...]
where the time goes in v1:
time: 194 us
  Pallas kernels  186 us (96%)
  other arithmetic  5.97 us (3%)
    pallas_call x1, Pallas kernels, body(): pl.pallas_call(functools.partial(kernel, L, T, NP), out_shape=(jax.ShapeD...  186 us
    convert_element_type x1, other arithmetic, body(): return (raw.astype(F32) * factor[0, :L, None, None]).astype(BF16)  5.97 us

profile of v1, /device:TPU:0, one launch (start us, length us, event | category | flops | bytes accessed | tf_op | source)
XLA Modules:
  0.0 194.1 jit_solution(4366553927451955874)
XLA Ops:
  1.3 186.1 %shard_map.73 = (bf16[8,256,1024]{2,1,0:T(8,128)(2,1)}, f32[8,128]{1,0:T(8,128)}) custom-call(bf16[8,256,1024]{2,1,0:T(8,128)(2,1)} %g.1, bf16[256,256]{1,0:T(8,128)(2,1)} %bitcast.9, bf16[2048,256]{1,0:T(8,128)(2,1)} %bitcast.8, f32[1,256]{1,0:T(1,128)} %reig.1, f32[1,256]{1,0:T(1,128)} %ceig.1, f32[1,1]{1,0:T(1,128)} %bitcast.6.resc, f32[1,1]{1,0:T(1,128)} %bitcast.7.cesc), custom_call_target="tpu_custom_call" | custom-call | tf_op jit(solution)/shard_map/pallas_call | solution.py:355
  187.4 0.7 slice_bitcast_fusion
  188.1 6.0 %multiply_convert_fusion = bf16[8,256,1024]{2,1,0:T(8,128)(2,1)} fusion(bf16[8,256,1024]{2,1,0:T(8,128)(2,1)} %get-tuple-element.7, f32[8]{0:T(128)S(1)} %slice_bitcast_fusion), kind=kLoop, calls=%fused_computation | loop fusion | flops 6291456 | bytes 8388640 | tf_op jit(solution)/shard_map/convert_element_type | solution.py:389

commit v2 on v1

v2 whole, which is shorter than its diff:
```python
import functools

import jax
import jax.numpy as jnp
from jax import lax
from jax.experimental import pallas as pl
from jax.experimental.pallas import tpu as pltpu
from jax.sharding import PartitionSpec as P

MESH = pl.DeviceIdType.MESH
F32 = jnp.float32
BF16 = jnp.bfloat16


def remote(src, dst, send, recv, axis, index):
    return pltpu.make_async_remote_copy(
        src_ref=src,
        dst_ref=dst,
        send_sem=send,
        recv_sem=recv,
        device_id={axis: index},
        device_id_type=MESH,
    )


def loop(lo, hi, fn):
    def step(i, carry):
        fn(i)
        return carry

    lax.fori_loop(lo, hi, step, 0)


def dot(a, b, dims=((1,), (0,))):
    return lax.dot_general(a, b, (dims, ((), ())), preferred_element_type=F32)


def quarter(x):
    return lax.rsqrt(jnp.sqrt(x))


def lanes(x):
    s = jnp.sum(x * x, axis=0, keepdims=True)
    out = s[:, 0:128]
    for k in range(1, x.shape[1] // 128):
        out = out + s[:, k * 128:(k + 1) * 128]
    return out


def kernel(
    L, T, NP,
    g_hbm, u, cols_hbm, reig, ceig, resc, cesc,
    raw, factor,
    g, uall, vall, vline, own, pin, qin, mout, mi, mid, lall, core_out, core_in, core_sum, cb,
    nsend, tile, nin,
    us, ur, bs, br, vs, vr, xs, xr, ms, mr, ks, kr, ls, lr, ps, pr, qs, qr, ns, nr, gs, cs,
):
    me = lax.axis_index("layer")
    t = lax.axis_index("tensor")
    W = g.shape[2]
    Cr = cols_hbm.shape[0]
    B = Cr // W
    BP = B // NP
    PR = Cr // NP
    K = u.shape[1]
    right, lft = t + 1, t - 1
    has_right, has_left = t < T - 1, t > 0
    inner = has_right & has_left
    far = jnp.maximum(t, T - 1 - t)

    here = me * T + t
    N = L * T

    def g_in(l):
        return pltpu.make_async_copy(g_hbm.at[l], g.at[l], gs.at[l])

    def cols_in(i):
        return pltpu.make_async_copy(cols_hbm.at[pl.ds(i * PR, PR)], vline.at[t, i], cs.at[i])

    for i in range(NP):
        cols_in(i).start()

    def greet(d):
        o = lax.rem(here + d, N)
        pl.semaphore_signal(
            barrier, inc=1, device_id={"layer": lax.div(o, T), "tensor": lax.rem(o, T)}, device_id_type=MESH)

    barrier = pltpu.get_barrier_semaphore()
    loop(1, N, greet)
    loop(0, L, lambda d: g_in(lax.rem(me - d + L, L)).start())

    row_base = quarter(resc[...])
    column_base = quarter(cesc[...])
    row_coef = quarter(reig[...] + resc[...]) - row_base
    dc = quarter(ceig[...] + cesc[...]) - column_base
    cb[me, 0:1, :] = row_coef * column_base
    cb[me, 1:2, :] = jnp.broadcast_to(row_base * column_base, (1, K))
    cb[me, 2:8, :] = jnp.broadcast_to(row_coef, (6, K))
    uall[me] = u[...]

    for i in range(NP):
        cols_in(i).wait()
    pl.semaphore_wait(barrier, N - 1)

    def layer_of(d):
        return lax.rem(me - d + L, L)

    def v_copy(src, c, i, side):
        return remote(src, vline.at[c, i], vs.at[side, c, i], vr.at[c, i], "tensor",
                      right if side == 0 else lft)

    def x_copy(src, slot, dst):
        return remote(src, vall.at[slot], xs.at[dst], xr.at[slot], "layer", dst)

    def u_copy(slot, dst):
        return remote(u, uall.at[slot], us.at[dst], ur.at[slot], "layer", dst)

    def b_copy(slot, dst):
        return remote(cb.at[me], cb.at[slot], bs.at[dst], br.at[slot], "layer", dst)

    def m_copy(slot, dst):
        return remote(mout.at[dst], mi.at[slot], ms.at[dst], mr.at[slot], "layer", dst)

    def l_copy(slot, dst):
        return remote(lall.at[me], lall.at[slot], ls.at[dst], lr.at[slot], "layer", dst)

    def k_copy(src, side):
        return remote(src, core_in.at[side], ks.at[side], kr.at[side], "tensor", right if side == 0 else lft)

    def p_copy(src, d):
        return remote(src, pin.at[d], ps.at[d], pr.at[d], "tensor", right)

    def q_copy(src, d):
        return remote(src, qin.at[d], qs.at[d], qr.at[d], "tensor", lft)

    for i in range(NP):
        pl.when(has_right)(lambda i=i: v_copy(vline.at[t, i], t, i, 0).start())
        pl.when(has_left)(lambda i=i: v_copy(vline.at[t, i], t, i, 1).start())

    def send_basis(d):
        dst = lax.rem(me + d, L)
        u_copy(me, dst).start()
        b_copy(me, dst).start()

    loop(1, L, send_basis)

    def spread(c, i):
        def rows(b):
            return vline.at[c, i, pl.ds(pl.multiple_of(b * W, 128), W)]

        def one(b):
            dst = c * B + i * BP + b
            pl.when(dst != me)(lambda: x_copy(rows(b), me, dst).start())

            @pl.when(dst == me)
            def _():
                vall[me] = rows(b)[...]

        loop(0, BP, one)

    for i in range(NP):
        spread(t, i)

    @pl.when(t == 0)
    def _():
        loop(0, L, lambda d: pin.__setitem__(d, jnp.zeros(pin.shape[1:], BF16)))

    @pl.when(t == T - 1)
    def _():
        loop(0, L, lambda d: qin.__setitem__(d, jnp.zeros(qin.shape[1:], BF16)))

    def project(d):
        l = layer_of(d)

        @pl.when(d > 0)
        def _():
            u_copy(l, l).wait_recv()
            b_copy(l, l).wait_recv()

        g_in(l).wait()
        block = g[l]
        own[d] = dot(uall[l], block, ((0,), (0,))).astype(BF16)
        nsend[0, pl.ds(l, 1), :] = lanes(block.astype(F32))

    loop(0, L, project)

    def end_send(d):
        @pl.when((d >= 0) & (d < L))
        def _():
            pl.when(t == 0)(lambda: p_copy(own.at[d], d).start())
            pl.when(t == T - 1)(lambda: q_copy(own.at[d], d).start())

    def core_pass(side, onward):
        k_copy(core_out, side).wait_recv()

        @pl.when(onward)
        def _():
            core_sum[side] = (core_in[side].astype(F32) + core_out[...].astype(F32)).astype(BF16)
            k_copy(core_sum.at[side], side).start()

    def forward(s, tau, copy, buf, side):
        d = s - NP * tau - 1
        ok = (d >= 0) & (d < L) & inner
        pl.when(ok)(lambda: copy(own.at[0], d).wait_recv())
        pl.when(inner & (s == at_core_end + tau))(lambda: core_pass(side, True))

        @pl.when(ok)
        def _():
            buf[d] = (buf[d].astype(F32) + own[d].astype(F32)).astype(BF16)
            copy(buf.at[d], d).start()

    def relay(h, i):
        for side, c, ok, onward in ((0, t - h, t - h >= 0, has_right), (1, t + h, t + h < T, has_left)):
            @pl.when(ok)
            def _(side=side, c=c, onward=onward):
                v_copy(vline.at[c, i], c, i, side).wait_recv()
                pl.when(onward)(lambda: v_copy(vline.at[c, i], c, i, side).start())
                spread(c, i)

    def middle(d):
        l = layer_of(d)
        pl.when(d > 0)(lambda: x_copy(vall.at[l], l, l).wait_recv())
        m = dot(g[l], vall[l]).astype(BF16)

        @pl.when(d == 0)
        def _():
            mi[me] = m

        @pl.when(d > 0)
        def _():
            mout[l] = m
            m_copy(me, l).start()

    def gather_middle():
        total = mi[me].astype(F32)
        mid[...] = total

        def add(d):
            l = layer_of(d)
            m_copy(l, l).wait_recv()
            mid[...] += mi[l].astype(F32)

        loop(1, L, add)
        core_out[...] = dot(u[...], mid[...].astype(BF16), ((0,), (0,))).astype(BF16)

        @pl.when(t == 0)
        def _():
            core_in[0] = jnp.zeros(core_out.shape, BF16)
            k_copy(core_out, 0).start()

        @pl.when(t == T - 1)
        def _():
            core_in[1] = jnp.zeros(core_out.shape, BF16)
            k_copy(core_out, 1).start()

    def make_left():
        pl.when(t == 0)(lambda: core_pass(1, False))
        pl.when(t == T - 1)(lambda: core_pass(0, False))
        core = core_in[0].astype(F32) + core_in[1].astype(F32) + core_out[...].astype(F32)
        core = (core * jnp.transpose(cb[me])[:, 2:3]).astype(BF16)
        mixed = row_base * mid[...] + dot(u[...], core)
        lall[me] = (mixed * dc).astype(BF16)
        loop(1, L, lambda d: l_copy(me, lax.rem(me + d, L)).start())

    sign = jnp.where(inner, -1.0, 1.0).astype(F32)

    def emit(d):
        l = layer_of(d)
        pl.when(d > 0)(lambda: l_copy(l, l).wait_recv())
        pl.when(t == T - 1)(lambda: p_copy(own.at[d], d).wait_recv())
        pl.when(t == 0)(lambda: q_copy(own.at[d], d).wait_recv())
        total = pin[d].astype(F32) + qin[d].astype(F32) + sign * own[d].astype(F32)
        scaled = (total * jnp.transpose(cb[l])[:, 0:1]).astype(BF16)
        x = cb[l, 1:2, 0:1] * g[l].astype(F32)
        x = x + dot(uall[l], scaled)
        x = x + dot(lall[l], vall[l], ((1,), (1,)))
        raw[l] = x.astype(BF16)
        nsend[1, pl.ds(l, 1), :] = lanes(x)

    blk = lax.div(lax.rem(me, B), BP)
    dist = jnp.abs(t - lax.div(me, B))
    first = jnp.where(dist == 0, 1, NP * (dist - 1) + blk + 1)
    per = max(L // 4, 1)
    at_core = NP * far + 4
    at_core_end = NP * (T - 1) + 3
    last = max(NP * (T - 2) + L, at_core_end + T - 2, NP * (T - 1) + 4)

    def step(s):
        pl.when(s <= NP * (T - 1))(
            lambda: relay(lax.div(s - 1, NP) + 1, lax.rem(s - 1, NP)))
        end_send(s - 1)
        forward(s, t, p_copy, pin, 0)
        forward(s, T - 1 - t, q_copy, qin, 1)
        loop(jnp.clip(per * (s - first - 1), 0, L), jnp.clip(per * (s - first), 0, L), middle)
        pl.when(s == at_core)(gather_middle)

    loop(1, last + 1, step)
    make_left()
    loop(0, L, emit)

    tile[...] = jnp.zeros_like(tile)
    tile[0:2, 0:L] = jnp.sum(nsend[...], axis=2)

    def n_copy(slot, dst):
        return pltpu.make_async_remote_copy(
            src_ref=tile, dst_ref=nin.at[slot], send_sem=ns.at[dst], recv_sem=nr.at[slot],
            device_id={"layer": lax.div(dst, T), "tensor": lax.rem(dst, T)}, device_id_type=MESH)

    loop(1, N, lambda d: n_copy(here, lax.rem(here + d, N)).start())
    nin[here] = tile[...]

    def finish(d):
        o = lax.rem(here + d, N)
        n_copy(o, o).wait_recv()

    loop(1, N, finish)
    tot = jnp.sum(nin[...], axis=0)
    fac = jnp.broadcast_to(jnp.sqrt((tot[0:1] + 1.0) / (tot[1:2] + 1.0)), (8, 128))
    factor[...] = jnp.broadcast_to(jnp.transpose(fac)[0:L, 0:1], factor.shape)

    def drain_layer(d):
        j = lax.rem(me + d, L)
        u_copy(me, j).wait_send()
        b_copy(me, j).wait_send()
        x_copy(vall.at[me], me, j).wait_send()
        m_copy(me, j).wait_send()
        l_copy(me, j).wait_send()

    loop(1, L, drain_layer)

    pl.when(has_right)(lambda: k_copy(core_out, 0).wait_send())
    pl.when(has_left)(lambda: k_copy(core_out, 1).wait_send())

    def drain_norm(d):
        o = lax.rem(here + d, N)
        n_copy(here, o).wait_send()

    loop(1, N, drain_norm)

    def drain_line(d):
        pl.when(has_right)(lambda: p_copy(own.at[d], d).wait_send())
        pl.when(has_left)(lambda: q_copy(own.at[d], d).wait_send())

    loop(0, L, drain_line)

    def drain_v(c):
        for i in range(NP):
            pl.when((c <= t) & has_right)(lambda i=i: v_copy(vline.at[c, i], c, i, 0).wait_send())
            pl.when((c >= t) & has_left)(lambda i=i: v_copy(vline.at[c, i], c, i, 1).wait_send())

    loop(0, T, drain_v)


def scale_kernel(raw, factor, out, buf, sem):
    def one(l):
        buf[l] = (raw[l].astype(F32) * factor[pl.ds(l, 1), 0:1]).astype(BF16)
        pltpu.make_async_copy(buf.at[l], out.at[l], sem.at[l]).start()

    L = raw.shape[0]
    loop(0, L, one)
    loop(0, L, lambda l: pltpu.make_async_copy(buf.at[l], out.at[l], sem.at[l]).wait())


def solution(mesh):
    L, T = mesh.shape["layer"], mesh.shape["tensor"]
    NP = 2

    def body(gradient, row_basis, column_basis, row_eigen, column_eigen, row_escape, column_escape):
        _, r, W = gradient.shape
        _, Cr, K = column_basis.shape
        vmem = pl.BlockSpec(memory_space=pltpu.VMEM)
        hbm = pl.BlockSpec(memory_space=pl.ANY)
        chunk = pltpu.VMEM((L, K, W), BF16)
        small = pltpu.VMEM((L, r, K), BF16)
        sem = pltpu.SemaphoreType.DMA
        raw, factor = pl.pallas_call(
            functools.partial(kernel, L, T, NP),
            out_shape=(pltpu.VMEM((L, r, W), BF16), pltpu.VMEM((L, 128), F32)),
            in_specs=[hbm, vmem, hbm, vmem, vmem, vmem, vmem],
            out_specs=(vmem, vmem),
            scratch_shapes=[
                pltpu.VMEM((L, r, W), BF16),
                small,
                pltpu.VMEM((L, W, K), BF16),
                pltpu.VMEM((T, NP, Cr // NP, K), BF16),
                chunk, chunk, chunk,
                small, small,
                pltpu.VMEM((r, K), F32),
                small,
                pltpu.VMEM((K, K), BF16),
                pltpu.VMEM((2, K, K), BF16),
                pltpu.VMEM((2, K, K), BF16),
                pltpu.VMEM((L, 8, K), F32),
                pltpu.VMEM((2, L, 128), F32),
                pltpu.VMEM((8, 128), F32),
                pltpu.VMEM((L * T, 8, 128), F32),
                sem((L,)), sem((L,)),
                sem((L,)), sem((L,)),
                sem((2, T, NP)), sem((T, NP)),
                sem((L,)), sem((L,)),
                sem((L,)), sem((L,)),
                sem((2,)), sem((2,)),
                sem((L,)), sem((L,)),
                sem((L,)), sem((L,)),
                sem((L,)), sem((L,)),
                sem((L * T,)), sem((L * T,)),
                sem((L,)), sem((NP,)),
            ],
            compiler_params=pltpu.CompilerParams(
                collective_id=0, has_side_effects=True, vmem_limit_bytes=67043328 - 2 * L * r * W - 256 * 1024),
        )(gradient, row_basis[0], column_basis[0], row_eigen, column_eigen,
          row_escape[:, None], column_escape[:, None])
        return pl.pallas_call(
            scale_kernel,
            out_shape=jax.ShapeDtypeStruct((L, r, W), BF16),
            in_specs=[vmem, vmem],
            out_specs=hbm,
            scratch_shapes=[pltpu.VMEM((L, r, W), BF16), sem((L,))],
            compiler_params=pltpu.CompilerParams(vmem_limit_bytes=32 * 1024 * 1024),
        )(raw, factor)

    in_specs = (
        P(None, "tensor", "layer"),
        P("layer", "tensor", None),
        P("layer", "tensor", None),
        P("layer", None),
        P("layer", None),
        P("layer"),
        P("layer"),
    )
    out_specs = P(None, "tensor", "layer")
    return jax.shard_map(body, mesh=mesh, in_specs=in_specs, out_specs=out_specs, check_vma=False)
```

time: 194 us -> 182 us (0.938)
  other arithmetic: 5.97 us -> 0 us
  Pallas kernels: 186 us -> 181 us
    convert_element_type x1 -> x0, other arithmetic: 5.97 us -> none  [body(): return (raw.astype(F32) * factor[0, :L, None, None]).astype(BF16)]
    pallas_call x1 -> x2, Pallas kernels: 186 us -> 181 us  [the longest x1 178 us: body(): pl.pallas_call(functools.partial(kernel, L, T, NP), out_shape=(pltpu.VMEM...]
where the time goes in v2:
time: 182 us
  Pallas kernels  181 us (99%)
    pallas_call x1, Pallas kernels, body(): pl.pallas_call(functools.partial(kernel, L, T, NP), out_shape=(pltpu.VMEM...  178 us

profile of v2, /device:TPU:0, one launch (start us, length us, event | category | flops | bytes accessed | tf_op | source)
XLA Modules:
  0.0 181.9 jit_solution(2510619370884347798)
XLA Ops:
  1.3 178.3 %shard_map.73 = (bf16[8,256,1024]{2,1,0:T(8,128)(2,1)S(1)}, f32[8,128]{1,0:T(8,128)S(1)}) custom-call(bf16[8,256,1024]{2,1,0:T(8,128)(2,1)} %g_hbm.1, bf16[256,256]{1,0:T(8,128)(2,1)} %bitcast.7, bf16[2048,256]{1,0:T(8,128)(2,1)} %bitcast.6, f32[1,256]{1,0:T(1,128)} %reig.1, f32[1,256]{1,0:T(1,128)} %ceig.1, f32[1,1]{1,0:T(1,128)} %bitcast.4.resc, ...), custom_call_target="tpu_custom_call" | custom-call | tf_op jit(solution)/shard_map/pallas_call | solution.py:376
  179.7 2.3 %shard_map.74 = bf16[8,256,1024]{2,1,0:T(8,128)(2,1)} custom-call(bf16[8,256,1024]{2,1,0:T(8,128)(2,1)S(1)} %get-tuple-element.7.raw, f32[8,128]{1,0:T(8,128)S(1)} %get-tuple-element.8.factor), custom_call_target="tpu_custom_call" | custom-call | tf_op jit(solution)/shard_map/pallas_call | solution.py:413

commit v3 on v2

--- a/solution.py
+++ b/solution.py
@@ -52,21 +52,18 @@
     g_hbm, u, cols_hbm, reig, ceig, resc, cesc,
     raw, factor,
     g, uall, vall, vline, own, pin, qin, mout, mi, mid, lall, core_out, core_in, core_sum, cb,
-    nsend, tile, nin,
-    us, ur, bs, br, vs, vr, xs, xr, ms, mr, ks, kr, ls, lr, ps, pr, qs, qr, ns, nr, gs, cs,
+    guest_g, guest_u, guest_l, guest_x, guest_n, nsend, tile, nin,
+    us, ur, bs, br, vs, vr, xs, xr, ms, mr, ks, kr, ls, lr, ps, pr, qs, qr, ns, nr, hs, hr, gs, cs,
 ):
     me = lax.axis_index("layer")
     t = lax.axis_index("tensor")
     W = g.shape[2]
-    Cr = cols_hbm.shape[0]
-    B = Cr // W
-    BP = B // NP
-    PR = Cr // NP
     K = u.shape[1]
     right, lft = t + 1, t - 1
     has_right, has_left = t < T - 1, t > 0
     inner = has_right & has_left
     far = jnp.maximum(t, T - 1 - t)
+    n_left, n_right = t, T - 1 - t
 
     here = me * T + t
     N = L * T
@@ -75,7 +72,7 @@
         return pltpu.make_async_copy(g_hbm.at[l], g.at[l], gs.at[l])
 
     def cols_in(i):
-        return pltpu.make_async_copy(cols_hbm.at[pl.ds(i * PR, PR)], vline.at[t, i], cs.at[i])
+        return pltpu.make_async_copy(cols_hbm.at[pl.ds(i * W, W)], vline.at[t, i], cs.at[i])
 
     for i in range(NP):
         cols_in(i).start()
@@ -87,8 +84,9 @@
 
     barrier = pltpu.get_barrier_semaphore()
     loop(1, N, greet)
-    loop(0, L, lambda d: g_in(lax.rem(me - d + L, L)).start())
-
+    loop(0, L, lambda d: g_in(lax.rem(me + d, L)).start())
+
+    tile[...] = jnp.zeros_like(tile)
     row_base = quarter(resc[...])
     column_base = quarter(cesc[...])
     row_coef = quarter(reig[...] + resc[...]) - row_base
@@ -103,7 +101,7 @@
     pl.semaphore_wait(barrier, N - 1)
 
     def layer_of(d):
-        return lax.rem(me - d + L, L)
+        return lax.rem(me + d, L)
 
     def v_copy(src, c, i, side):
         return remote(src, vline.at[c, i], vs.at[side, c, i], vr.at[c, i], "tensor",
@@ -133,33 +131,28 @@
     def q_copy(src, d):
         return remote(src, qin.at[d], qs.at[d], qr.at[d], "tensor", lft)
 
-    for i in range(NP):
-        pl.when(has_right)(lambda i=i: v_copy(vline.at[t, i], t, i, 0).start())
-        pl.when(has_left)(lambda i=i: v_copy(vline.at[t, i], t, i, 1).start())
+    def send_own(i, side):
+        v_copy(vline.at[t, i], t, i, side).start()
+
+    pl.when(has_right)(lambda: loop(0, jnp.where(has_left, 1, NP), lambda i: send_own(i, 0)))
+    pl.when(has_left)(lambda: loop(0, jnp.where(has_right, 1, NP), lambda i: send_own(i, 1)))
 
     def send_basis(d):
-        dst = lax.rem(me + d, L)
+        dst = lax.rem(me - d + L, L)
         u_copy(me, dst).start()
         b_copy(me, dst).start()
 
     loop(1, L, send_basis)
 
     def spread(c, i):
-        def rows(b):
-            return vline.at[c, i, pl.ds(pl.multiple_of(b * W, 128), W)]
-
-        def one(b):
-            dst = c * B + i * BP + b
-            pl.when(dst != me)(lambda: x_copy(rows(b), me, dst).start())
-
-            @pl.when(dst == me)
-            def _():
-                vall[me] = rows(b)[...]
-
-        loop(0, BP, one)
-
-    for i in range(NP):
-        spread(t, i)
+        dst = c * NP + i
+        pl.when(dst != me)(lambda: x_copy(vline.at[c, i], me, dst).start())
+
+        @pl.when(dst == me)
+        def _():
+            vall[me] = vline[c, i]
+
+    loop(0, NP, lambda i: spread(t, i))
 
     @pl.when(t == 0)
     def _():
@@ -207,15 +200,19 @@
         @pl.when(ok)
         def _():
             buf[d] = (buf[d].astype(F32) + own[d].astype(F32)).astype(BF16)
-            copy(buf.at[d], d).start()
-
-    def relay(h, i):
-        for side, c, ok, onward in ((0, t - h, t - h >= 0, has_right), (1, t + h, t + h < T, has_left)):
-            @pl.when(ok)
-            def _(side=side, c=c, onward=onward):
-                v_copy(vline.at[c, i], c, i, side).wait_recv()
-                pl.when(onward)(lambda: v_copy(vline.at[c, i], c, i, side).start())
-                spread(c, i)
+            pl.when((d < L - 1) | (tau < T - 2))(lambda: copy(buf.at[d], d).start())
+
+    def relay(s, n, way, side, onward):
+        near = jnp.maximum(n, 1)
+        i, h = lax.div(s - 1, near), lax.rem(s - 1, near) + 1
+        c = t + way * h
+
+        @pl.when(s <= NP * n)
+        def _():
+            v_copy(vline.at[c, i], c, i, side).wait_recv()
+            pl.when(onward)(lambda: v_copy(vline.at[c, i], c, i, side).start())
+            pl.when(onward & (h == n) & (i + 1 < NP))(lambda: send_own(i + 1, side))
+            spread(c, i)
 
     def middle(d):
         l = layer_of(d)
@@ -254,8 +251,6 @@
             k_copy(core_out, 1).start()
 
     def make_left():
-        pl.when(t == 0)(lambda: core_pass(1, False))
-        pl.when(t == T - 1)(lambda: core_pass(0, False))
         core = core_in[0].astype(F32) + core_in[1].astype(F32) + core_out[...].astype(F32)
         core = (core * jnp.transpose(cb[me])[:, 2:3]).astype(BF16)
         mixed = row_base * mid[...] + dot(u[...], core)
@@ -264,42 +259,87 @@
 
     sign = jnp.where(inner, -1.0, 1.0).astype(F32)
 
+    def pushed(d):
+        total = pin[d].astype(F32) + qin[d].astype(F32) + sign * own[d].astype(F32)
+        return (total * jnp.transpose(cb[layer_of(d)])[:, 0:1]).astype(BF16)
+
+    def update(l, block, basis, scaled, left):
+        x = cb[l, 1:2, 0:1] * block.astype(F32)
+        x = x + dot(basis, scaled)
+        return x + dot(left, vall[l], ((1,), (1,)))
+
     def emit(d):
         l = layer_of(d)
         pl.when(d > 0)(lambda: l_copy(l, l).wait_recv())
         pl.when(t == T - 1)(lambda: p_copy(own.at[d], d).wait_recv())
         pl.when(t == 0)(lambda: q_copy(own.at[d], d).wait_recv())
-        total = pin[d].astype(F32) + qin[d].astype(F32) + sign * own[d].astype(F32)
-        scaled = (total * jnp.transpose(cb[l])[:, 0:1]).astype(BF16)
-        x = cb[l, 1:2, 0:1] * g[l].astype(F32)
-        x = x + dot(uall[l], scaled)
-        x = x + dot(lall[l], vall[l], ((1,), (1,)))
+        x = update(l, g[l], uall[l], pushed(d), lall[l])
         raw[l] = x.astype(BF16)
         nsend[1, pl.ds(l, 1), :] = lanes(x)
 
-    blk = lax.div(lax.rem(me, B), BP)
-    dist = jnp.abs(t - lax.div(me, B))
-    first = jnp.where(dist == 0, 1, NP * (dist - 1) + blk + 1)
-    per = max(L // 4, 1)
-    at_core = NP * far + 4
-    at_core_end = NP * (T - 1) + 3
-    last = max(NP * (T - 2) + L, at_core_end + T - 2, NP * (T - 1) + 4)
+    final = L - 1
+    lf = layer_of(final)
+
+    def h_copies(side):
+        to = lax.rem(t + (1 if side == 0 else T - 1), T)
+        return [
+            remote(src, dst, hs.at[k], hr.at[k], "tensor", to)
+            for k, (src, dst) in enumerate(((g.at[lf], guest_g), (uall.at[lf], guest_u), (lall.at[lf], guest_l)))]
+
+    def guest_emit():
+        for copy in h_copies(0):
+            copy.wait_recv()
+        x = update(lf, guest_g[...], guest_u[...], pushed(final), guest_l[...])
+        guest_x[...] = x.astype(BF16)
+        guest_n[...] = lanes(x)
+        pl.when(t == T - 2)(lambda: p_copy(guest_x, final).start())
+        pl.when(t == 1)(lambda: q_copy(guest_x, final).start())
+
+    blk = lax.rem(me, NP)
+    home = lax.div(me, NP)
+    dist = jnp.abs(t - home)
+    first = jnp.where(dist == 0, 2 * blk + 3, blk * jnp.where(home < t, n_left, n_right) + dist + 2)
+    at_core = NP * far + 2
+    at_core_end = NP * (T - 1) + 2
+    last = max(NP * (T - 2) + L, at_core_end + T - 2, NP * (T - 1) + 2, 2 * NP + 1)
 
     def step(s):
-        pl.when(s <= NP * (T - 1))(
-            lambda: relay(lax.div(s - 1, NP) + 1, lax.rem(s - 1, NP)))
-        end_send(s - 1)
+        relay(s, n_left, -1, 0, has_right)
+        relay(s, n_right, 1, 1, has_left)
+        pl.when(s < L)(lambda: end_send(s - 1))
         forward(s, t, p_copy, pin, 0)
         forward(s, T - 1 - t, q_copy, qin, 1)
-        loop(jnp.clip(per * (s - first - 1), 0, L), jnp.clip(per * (s - first), 0, L), middle)
-        pl.when(s == at_core)(gather_middle)
-
+        loop(jnp.where(s == first, 0, L), L, middle)
+
+        @pl.when(s == at_core)
+        def _():
+            gather_middle()
+            end_send(L - 1)
+
+        pl.when(inner & (s == at_core_end + T - 2))(make_left)
+
+    guest_n[...] = jnp.zeros_like(guest_n)
+    nsend[1, pl.ds(lf, 1), :] = jnp.zeros((1, 128), F32)
     loop(1, last + 1, step)
-    make_left()
-    loop(0, L, emit)
-
-    tile[...] = jnp.zeros_like(tile)
-    tile[0:2, 0:L] = jnp.sum(nsend[...], axis=2)
+
+    def end_left(side):
+        copies = h_copies(side)
+        copies[0].start()
+        copies[1].start()
+        core_pass(1 - side, False)
+        make_left()
+        l_copy(lf, lf).wait_recv()
+        copies[2].start()
+
+    pl.when(t == 0)(lambda: end_left(0))
+    pl.when(t == T - 1)(lambda: end_left(1))
+    pl.when((t == 1) | (t == T - 2))(guest_emit)
+    loop(0, jnp.where(inner, L, L - 1), emit)
+
+    nsend[1, pl.ds(lf, 1), :] = nsend[1, pl.ds(lf, 1), :] + guest_n[...]
+    sums = jnp.sum(nsend[...], axis=2)
+    tile[0:1, 0:L] = sums[0:1]
+    tile[0:1, L:2 * L] = sums[1:2]
 
     def n_copy(slot, dst):
         return pltpu.make_async_remote_copy(
@@ -308,15 +348,6 @@
 
     loop(1, N, lambda d: n_copy(here, lax.rem(here + d, N)).start())
     nin[here] = tile[...]
-
-    def finish(d):
-        o = lax.rem(here + d, N)
-        n_copy(o, o).wait_recv()
-
-    loop(1, N, finish)
-    tot = jnp.sum(nin[...], axis=0)
-    fac = jnp.broadcast_to(jnp.sqrt((tot[0:1] + 1.0) / (tot[1:2] + 1.0)), (8, 128))
-    factor[...] = jnp.broadcast_to(jnp.transpose(fac)[0:L, 0:1], factor.shape)
 
     def drain_layer(d):
         j = lax.rem(me + d, L)
@@ -331,12 +362,6 @@
     pl.when(has_right)(lambda: k_copy(core_out, 0).wait_send())
     pl.when(has_left)(lambda: k_copy(core_out, 1).wait_send())
 
-    def drain_norm(d):
-        o = lax.rem(here + d, N)
-        n_copy(here, o).wait_send()
-
-    loop(1, N, drain_norm)
-
     def drain_line(d):
         pl.when(has_right)(lambda: p_copy(own.at[d], d).wait_send())
         pl.when(has_left)(lambda: q_copy(own.at[d], d).wait_send())
@@ -350,6 +375,37 @@
 
     loop(0, T, drain_v)
 
+    for side, end in ((0, 0), (1, T - 1)):
+        @pl.when(t == end)
+        def _(side=side):
+            for copy in h_copies(side):
+                copy.wait_send()
+
+    def finish(d):
+        o = lax.rem(here + d, N)
+        n_copy(o, o).wait_recv()
+
+    loop(1, N, finish)
+    tot = jnp.sum(nin[...], axis=0)
+    fac = jnp.sqrt((tot[:, 0:L] + 1.0) / (tot[:, L:2 * L] + 1.0))
+    factor[...] = jnp.broadcast_to(jnp.transpose(jnp.broadcast_to(fac, (8, L)))[:, 0:1], factor.shape)
+
+    def drain_norm(d):
+        o = lax.rem(here + d, N)
+        n_copy(here, o).wait_send()
+
+    loop(1, N, drain_norm)
+
+    @pl.when(t == T - 1)
+    def _():
+        p_copy(own.at[final], final).wait_recv()
+        raw[lf] = pin[final]
+
+    @pl.when(t == 0)
+    def _():
+        q_copy(own.at[final], final).wait_recv()
+        raw[lf] = qin[final]
+
 
 def scale_kernel(raw, factor, out, buf, sem):
     def one(l):
@@ -363,7 +419,7 @@
 
 def solution(mesh):
     L, T = mesh.shape["layer"], mesh.shape["tensor"]
-    NP = 2
+    NP = L // T
 
     def body(gradient, row_basis, column_basis, row_eigen, column_eigen, row_escape, column_escape):
         _, r, W = gradient.shape
@@ -391,9 +447,14 @@
                 pltpu.VMEM((2, K, K), BF16),
                 pltpu.VMEM((2, K, K), BF16),
                 pltpu.VMEM((L, 8, K), F32),
+                pltpu.VMEM((r, W), BF16),
+                pltpu.VMEM((r, K), BF16),
+                pltpu.VMEM((r, K), BF16),
+                pltpu.VMEM((r, W), BF16),
+                pltpu.VMEM((1, 128), F32),
                 pltpu.VMEM((2, L, 128), F32),
-                pltpu.VMEM((8, 128), F32),
-                pltpu.VMEM((L * T, 8, 128), F32),
+                pltpu.VMEM((1, 128), F32),
+                pltpu.VMEM((L * T, 1, 128), F32),
                 sem((L,)), sem((L,)),
                 sem((L,)), sem((L,)),
                 sem((2, T, NP)), sem((T, NP)),
@@ -404,6 +465,7 @@
                 sem((L,)), sem((L,)),
                 sem((L,)), sem((L,)),
                 sem((L * T,)), sem((L * T,)),
+                sem((3,)), sem((3,)),
                 sem((L,)), sem((NP,)),
             ],
             compiler_params=pltpu.CompilerParams(

time: 182 us -> 181 us (level)
  no operation moved by 1% of the time
where the time goes in v3:
time: 181 us
  Pallas kernels  180 us (99%)
    pallas_call x1, Pallas kernels, body(): pl.pallas_call(functools.partial(kernel, L, T, NP), out_shape=(pltpu.VMEM...  177 us

profile of v3, /device:TPU:0, one launch (start us, length us, event | category | flops | bytes accessed | tf_op | source)
XLA Modules:
  0.0 181.0 jit_solution(7545346886211311112)
XLA Ops:
  1.3 177.5 %shard_map.73 = (bf16[8,256,1024]{2,1,0:T(8,128)(2,1)S(1)}, f32[8,128]{1,0:T(8,128)S(1)}) custom-call(bf16[8,256,1024]{2,1,0:T(8,128)(2,1)} %g_hbm.1, bf16[256,256]{1,0:T(8,128)(2,1)} %bitcast.7, bf16[2048,256]{1,0:T(8,128)(2,1)} %bitcast.6, f32[1,256]{1,0:T(1,128)} %reig.1, f32[1,256]{1,0:T(1,128)} %ceig.1, f32[1,1]{1,0:T(1,128)} %bitcast.4.resc, ...), custom_call_target="tpu_custom_call" | custom-call | tf_op jit(solution)/shard_map/pallas_call | solution.py:432
  178.8 2.3 %shard_map.74 = bf16[8,256,1024]{2,1,0:T(8,128)(2,1)} custom-call(bf16[8,256,1024]{2,1,0:T(8,128)(2,1)S(1)} %get-tuple-element.7.raw, f32[8,128]{1,0:T(8,128)S(1)} %get-tuple-element.8.factor), custom_call_target="tpu_custom_call" | custom-call | tf_op jit(solution)/shard_map/pallas_call | solution.py:475

commit v4 on v3

--- a/solution.py
+++ b/solution.py
@@ -68,8 +68,7 @@
     here = me * T + t
     N = L * T
 
-    def g_in(l):
-        return pltpu.make_async_copy(g_hbm.at[l], g.at[l], gs.at[l])
+    g_in = pltpu.make_async_copy(g_hbm, g, gs)
 
     def cols_in(i):
         return pltpu.make_async_copy(cols_hbm.at[pl.ds(i * W, W)], vline.at[t, i], cs.at[i])
@@ -77,14 +76,14 @@
     for i in range(NP):
         cols_in(i).start()
 
-    def greet(d):
-        o = lax.rem(here + d, N)
-        pl.semaphore_signal(
-            barrier, inc=1, device_id={"layer": lax.div(o, T), "tensor": lax.rem(o, T)}, device_id_type=MESH)
+    def greet(axis, index):
+        pl.semaphore_signal(barrier, inc=1, device_id={axis: index}, device_id_type=MESH)
 
     barrier = pltpu.get_barrier_semaphore()
-    loop(1, N, greet)
-    loop(0, L, lambda d: g_in(lax.rem(me + d, L)).start())
+    pl.when(has_right)(lambda: greet("tensor", right))
+    pl.when(has_left)(lambda: greet("tensor", lft))
+    loop(1, L, lambda d: greet("layer", lax.rem(me + d, L)))
+    g_in.start()
 
     tile[...] = jnp.zeros_like(tile)
     row_base = quarter(resc[...])
@@ -98,44 +97,54 @@
 
     for i in range(NP):
         cols_in(i).wait()
-    pl.semaphore_wait(barrier, N - 1)
+    pl.semaphore_wait(barrier, L - 1 + jnp.where(inner, 2, 1))
 
     def layer_of(d):
         return lax.rem(me + d, L)
 
     def v_copy(src, c, i, side):
-        return remote(src, vline.at[c, i], vs.at[side, c, i], vr.at[c, i], "tensor",
+        return remote(src, vline.at[c, i], vs.at[side, c], vr.at[c, i], "tensor",
                       right if side == 0 else lft)
 
     def x_copy(src, slot, dst):
-        return remote(src, vall.at[slot], xs.at[dst], xr.at[slot], "layer", dst)
+        return remote(src, vall.at[slot], xs, xr.at[slot], "layer", dst)
 
     def u_copy(slot, dst):
-        return remote(u, uall.at[slot], us.at[dst], ur.at[slot], "layer", dst)
+        return remote(u, uall.at[slot], us, ur.at[slot], "layer", dst)
 
     def b_copy(slot, dst):
-        return remote(cb.at[me], cb.at[slot], bs.at[dst], br.at[slot], "layer", dst)
+        return remote(cb.at[me], cb.at[slot], bs, br.at[slot], "layer", dst)
 
     def m_copy(slot, dst):
-        return remote(mout.at[dst], mi.at[slot], ms.at[dst], mr.at[slot], "layer", dst)
+        return remote(mout.at[dst], mi.at[slot], ms, mr, "layer", dst)
 
     def l_copy(slot, dst):
-        return remote(lall.at[me], lall.at[slot], ls.at[dst], lr.at[slot], "layer", dst)
+        return remote(lall.at[me], lall.at[slot], ls, lr.at[slot], "layer", dst)
 
     def k_copy(src, side):
         return remote(src, core_in.at[side], ks.at[side], kr.at[side], "tensor", right if side == 0 else lft)
 
     def p_copy(src, d):
-        return remote(src, pin.at[d], ps.at[d], pr.at[d], "tensor", right)
+        return remote(src, pin.at[d], ps, pr.at[d], "tensor", right)
 
     def q_copy(src, d):
-        return remote(src, qin.at[d], qs.at[d], qr.at[d], "tensor", lft)
+        return remote(src, qin.at[d], qs, qr.at[d], "tensor", lft)
 
     def send_own(i, side):
         v_copy(vline.at[t, i], t, i, side).start()
 
-    pl.when(has_right)(lambda: loop(0, jnp.where(has_left, 1, NP), lambda i: send_own(i, 0)))
-    pl.when(has_left)(lambda: loop(0, jnp.where(has_right, 1, NP), lambda i: send_own(i, 1)))
+    def send_half(i, half, side):
+        rows = vline.at[t, i, pl.ds(half * (W // 2), W // 2)]
+        remote(rows, rows, vs.at[side, t], vr.at[t, i], "tensor", right if side == 0 else lft).start()
+
+    def send_first(side, onward, n):
+        @pl.when(onward)
+        def _():
+            loop(0, jnp.where(n > 0, 1, NP), lambda i: send_own(i, side))
+            pl.when((n > 0) & (NP > 1))(lambda: send_half(1, 0, side))
+
+    send_first(0, has_right, n_left)
+    send_first(1, has_left, n_right)
 
     def send_basis(d):
         dst = lax.rem(me - d + L, L)
@@ -152,8 +161,6 @@
         def _():
             vall[me] = vline[c, i]
 
-    loop(0, NP, lambda i: spread(t, i))
-
     @pl.when(t == 0)
     def _():
         loop(0, L, lambda d: pin.__setitem__(d, jnp.zeros(pin.shape[1:], BF16)))
@@ -170,12 +177,12 @@
             u_copy(l, l).wait_recv()
             b_copy(l, l).wait_recv()
 
-        g_in(l).wait()
         block = g[l]
         own[d] = dot(uall[l], block, ((0,), (0,))).astype(BF16)
         nsend[0, pl.ds(l, 1), :] = lanes(block.astype(F32))
 
-    loop(0, L, project)
+    g_in.wait()
+    project(0)
 
     def end_send(d):
         @pl.when((d >= 0) & (d < L))
@@ -211,7 +218,8 @@
         def _():
             v_copy(vline.at[c, i], c, i, side).wait_recv()
             pl.when(onward)(lambda: v_copy(vline.at[c, i], c, i, side).start())
-            pl.when(onward & (h == n) & (i + 1 < NP))(lambda: send_own(i + 1, side))
+            pl.when(onward & (h == 1) & (i + 1 < NP))(lambda: send_half(i + 1, 1, side))
+            pl.when(onward & (h == n) & (i + 2 < NP))(lambda: send_half(i + 2, 0, side))
             spread(c, i)
 
     def middle(d):
@@ -232,10 +240,10 @@
         total = mi[me].astype(F32)
         mid[...] = total
 
+        remote(mout.at[pl.ds(0, L - 1)], mi.at[pl.ds(0, L - 1)], ms, mr, "layer", me).wait_recv()
+
         def add(d):
-            l = layer_of(d)
-            m_copy(l, l).wait_recv()
-            mid[...] += mi[l].astype(F32)
+            mid[...] += mi[layer_of(d)].astype(F32)
 
         loop(1, L, add)
         core_out[...] = dot(u[...], mid[...].astype(BF16), ((0,), (0,))).astype(BF16)
@@ -298,15 +306,18 @@
     blk = lax.rem(me, NP)
     home = lax.div(me, NP)
     dist = jnp.abs(t - home)
-    first = jnp.where(dist == 0, 2 * blk + 3, blk * jnp.where(home < t, n_left, n_right) + dist + 2)
+    third = -(-L // 3)
+    first = jnp.where(dist == 0, 2 * blk + 4, blk * jnp.where(home < t, n_left, n_right) + dist + 2)
     at_core = NP * far + 2
     at_core_end = NP * (T - 1) + 2
-    last = max(NP * (T - 2) + L, at_core_end + T - 2, NP * (T - 1) + 2, 2 * NP + 1)
+    last = max(NP * (T - 2) + L, at_core_end + T - 2, NP * (T - 1) + 2, 2 * NP + 2)
 
     def step(s):
         relay(s, n_left, -1, 0, has_right)
         relay(s, n_right, 1, 1, has_left)
+        pl.when(s == 1)(lambda: loop(0, NP, lambda i: spread(t, i)))
         pl.when(s < L)(lambda: end_send(s - 1))
+        loop(jnp.clip(third * (s - 1) + 1, 1, L), jnp.clip(third * s + 1, 1, L), project)
         forward(s, t, p_copy, pin, 0)
         forward(s, T - 1 - t, q_copy, qin, 1)
         loop(jnp.where(s == first, 0, L), L, middle)
@@ -343,35 +354,27 @@
 
     def n_copy(slot, dst):
         return pltpu.make_async_remote_copy(
-            src_ref=tile, dst_ref=nin.at[slot], send_sem=ns.at[dst], recv_sem=nr.at[slot],
+            src_ref=tile, dst_ref=nin.at[slot], send_sem=ns, recv_sem=nr,
             device_id={"layer": lax.div(dst, T), "tensor": lax.rem(dst, T)}, device_id_type=MESH)
 
     loop(1, N, lambda d: n_copy(here, lax.rem(here + d, N)).start())
     nin[here] = tile[...]
 
-    def drain_layer(d):
-        j = lax.rem(me + d, L)
-        u_copy(me, j).wait_send()
-        b_copy(me, j).wait_send()
-        x_copy(vall.at[me], me, j).wait_send()
-        m_copy(me, j).wait_send()
-        l_copy(me, j).wait_send()
-
-    loop(1, L, drain_layer)
-
+    def sent(ref, sem, axis):
+        remote(ref, ref, sem, sem, axis, 0).wait_send()
+
+    most = pl.ds(0, L - 1)
+    for ref, sem in ((uall, us), (cb, bs), (vall, xs), (mout, ms), (lall, ls)):
+        sent(ref.at[most], sem, "layer")
     pl.when(has_right)(lambda: k_copy(core_out, 0).wait_send())
     pl.when(has_left)(lambda: k_copy(core_out, 1).wait_send())
 
-    def drain_line(d):
-        pl.when(has_right)(lambda: p_copy(own.at[d], d).wait_send())
-        pl.when(has_left)(lambda: q_copy(own.at[d], d).wait_send())
-
-    loop(0, L, drain_line)
+    pl.when(has_right)(lambda: sent(own, ps, "tensor"))
+    pl.when(has_left)(lambda: sent(own, qs, "tensor"))
 
     def drain_v(c):
-        for i in range(NP):
-            pl.when((c <= t) & has_right)(lambda i=i: v_copy(vline.at[c, i], c, i, 0).wait_send())
-            pl.when((c >= t) & has_left)(lambda i=i: v_copy(vline.at[c, i], c, i, 1).wait_send())
+        pl.when((c <= t) & has_right)(lambda: sent(vline.at[c], vs.at[0, c], "tensor"))
+        pl.when((c >= t) & has_left)(lambda: sent(vline.at[c], vs.at[1, c], "tensor"))
 
     loop(0, T, drain_v)
 
@@ -381,20 +384,13 @@
             for copy in h_copies(side):
                 copy.wait_send()
 
-    def finish(d):
-        o = lax.rem(here + d, N)
-        n_copy(o, o).wait_recv()
-
-    loop(1, N, finish)
+    arrived = remote(nin.at[pl.ds(0, N - 1)], nin.at[pl.ds(0, N - 1)], ns, nr, "layer", 0)
+    arrived.wait_recv()
     tot = jnp.sum(nin[...], axis=0)
     fac = jnp.sqrt((tot[:, 0:L] + 1.0) / (tot[:, L:2 * L] + 1.0))
     factor[...] = jnp.broadcast_to(jnp.transpose(jnp.broadcast_to(fac, (8, L)))[:, 0:1], factor.shape)
 
-    def drain_norm(d):
-        o = lax.rem(here + d, N)
-        n_copy(here, o).wait_send()
-
-    loop(1, N, drain_norm)
+    arrived.wait_send()
 
     @pl.when(t == T - 1)
     def _():
@@ -455,18 +451,18 @@
                 pltpu.VMEM((2, L, 128), F32),
                 pltpu.VMEM((1, 128), F32),
                 pltpu.VMEM((L * T, 1, 128), F32),
-                sem((L,)), sem((L,)),
-                sem((L,)), sem((L,)),
-                sem((2, T, NP)), sem((T, NP)),
-                sem((L,)), sem((L,)),
-                sem((L,)), sem((L,)),
+                sem, sem((L,)),
+                sem, sem((L,)),
+                sem((2, T)), sem((T, NP)),
+                sem, sem((L,)),
+                sem, sem,
                 sem((2,)), sem((2,)),
-                sem((L,)), sem((L,)),
-                sem((L,)), sem((L,)),
-                sem((L,)), sem((L,)),
-                sem((L * T,)), sem((L * T,)),
+                sem, sem((L,)),
+                sem, sem((L,)),
+                sem, sem((L,)),
+                sem, sem,
                 sem((3,)), sem((3,)),
-                sem((L,)), sem((NP,)),
+                sem, sem((NP,)),
             ],
             compiler_params=pltpu.CompilerParams(
                 collective_id=0, has_side_effects=True, vmem_limit_bytes=67043328 - 2 * L * r * W - 256 * 1024),

time: 181 us -> 175 us (0.967)
  Pallas kernels: 180 us -> 173 us
    pallas_call x1, Pallas kernels: 177 us -> 171 us  [body(): pl.pallas_call(functools.partial(kernel, L, T, NP), out_shape=(pltpu.VMEM...]
where the time goes in v4:
time: 175 us
  Pallas kernels  173 us (99%)
    pallas_call x1, Pallas kernels, body(): pl.pallas_call(functools.partial(kernel, L, T, NP), out_shape=(pltpu.VMEM...  171 us

profile of v4, /device:TPU:0, one launch (start us, length us, event | category | flops | bytes accessed | tf_op | source)
XLA Modules:
  0.0 174.6 jit_solution(5681871271267037548)
XLA Ops:
  1.3 171.0 %shard_map.73 = (bf16[8,256,1024]{2,1,0:T(8,128)(2,1)S(1)}, f32[8,128]{1,0:T(8,128)S(1)}) custom-call(bf16[8,256,1024]{2,1,0:T(8,128)(2,1)} %g_hbm.1, bf16[256,256]{1,0:T(8,128)(2,1)} %bitcast.7, bf16[2048,256]{1,0:T(8,128)(2,1)} %bitcast.6, f32[1,256]{1,0:T(1,128)} %reig.1, f32[1,256]{1,0:T(1,128)} %ceig.1, f32[1,1]{1,0:T(1,128)} %bitcast.4.resc, ...), custom_call_target="tpu_custom_call" | custom-call | tf_op jit(solution)/shard_map/pallas_call | solution.py:428
  172.3 2.3 %shard_map.74 = bf16[8,256,1024]{2,1,0:T(8,128)(2,1)} custom-call(bf16[8,256,1024]{2,1,0:T(8,128)(2,1)S(1)} %get-tuple-element.7.raw, f32[8,128]{1,0:T(8,128)S(1)} %get-tuple-element.8.factor), custom_call_target="tpu_custom_call" | custom-call | tf_op jit(solution)/shard_map/pallas_call | solution.py:471

commit v5 on v4

--- a/solution.py
+++ b/solution.py
@@ -49,11 +49,11 @@
 
 def kernel(
     L, T, NP,
-    g_hbm, u, cols_hbm, reig, ceig, resc, cesc,
-    raw, factor,
-    g, uall, vall, vline, own, pin, qin, mout, mi, mid, lall, core_out, core_in, core_sum, cb,
-    guest_g, guest_u, guest_l, guest_x, guest_n, nsend, tile, nin,
-    us, ur, bs, br, vs, vr, xs, xr, ms, mr, ks, kr, ls, lr, ps, pr, qs, qr, ns, nr, hs, hr, gs, cs,
+    g_hbm, u_hbm, cols_hbm, reig_hbm, ceig_hbm, resc_hbm, cesc_hbm,
+    raw,
+    g, u, reig, ceig, resc, cesc, uall, vall, vline, own, pin, qin, mout, mi, mid, lall, core_out, core_in, core_sum, cb,
+    guest_g, guest_u, guest_l, guest_x, guest_n, nsend, tile, nin, factor,
+    us, ur, bs, br, vs, vr, xs, xr, ms, mr, ks, kr, ls, lr, ps, pr, qs, qr, ns, nr, hs, hr, gs, cs, es,
 ):
     me = lax.axis_index("layer")
     t = lax.axis_index("tensor")
@@ -69,6 +69,8 @@
     N = L * T
 
     g_in = pltpu.make_async_copy(g_hbm, g, gs)
+    small_in = [pltpu.make_async_copy(src, dst, es.at[k]) for k, (src, dst) in enumerate((
+        (u_hbm, u), (reig_hbm, reig), (ceig_hbm, ceig), (resc_hbm, resc), (cesc_hbm, cesc)))]
 
     def cols_in(i):
         return pltpu.make_async_copy(cols_hbm.at[pl.ds(i * W, W)], vline.at[t, i], cs.at[i])
@@ -83,8 +85,61 @@
     pl.when(has_right)(lambda: greet("tensor", right))
     pl.when(has_left)(lambda: greet("tensor", lft))
     loop(1, L, lambda d: greet("layer", lax.rem(me + d, L)))
+    for copy in small_in:
+        copy.start()
     g_in.start()
-
+    for i in range(NP):
+        cols_in(i).wait()
+    pl.semaphore_wait(barrier, L - 1 + jnp.where(inner, 2, 1))
+
+    def layer_of(d):
+        return lax.rem(me + d, L)
+
+    def v_copy(src, c, i, side):
+        return remote(src, vline.at[c, i], vs.at[side, c], vr.at[c, i], "tensor",
+                      right if side == 0 else lft)
+
+    def x_copy(src, slot, dst):
+        return remote(src, vall.at[slot], xs, xr.at[slot], "layer", dst)
+
+    def u_copy(slot, dst):
+        return remote(u, uall.at[slot], us, ur.at[slot], "layer", dst)
+
+    def b_copy(slot, dst):
+        return remote(cb.at[me], cb.at[slot], bs, br.at[slot], "layer", dst)
+
+    def m_copy(slot, dst):
+        return remote(mout.at[dst], mi.at[slot], ms, mr, "layer", dst)
+
+    def l_copy(slot, dst):
+        return remote(lall.at[me], lall.at[slot], ls, lr.at[slot], "layer", dst)
+
+    def k_copy(src, side):
+        return remote(src, core_in.at[side], ks.at[side], kr.at[side], "tensor", right if side == 0 else lft)
+
+    def p_copy(src, d):
+        return remote(src, pin.at[d], ps, pr.at[d], "tensor", right)
+
+    def q_copy(src, d):
+        return remote(src, qin.at[d], qs, qr.at[d], "tensor", lft)
+
+    def send_own(i, side):
+        v_copy(vline.at[t, i], t, i, side).start()
+
+    def send_half(i, half, side):
+        rows = vline.at[t, i, pl.ds(half * (W // 2), W // 2)]
+        remote(rows, rows, vs.at[side, t], vr.at[t, i], "tensor", right if side == 0 else lft).start()
+
+    def send_first(side, onward, n):
+        @pl.when(onward)
+        def _():
+            loop(0, jnp.where(n > 0, 1, NP), lambda i: send_own(i, side))
+            pl.when((n > 0) & (NP > 1))(lambda: send_half(1, 0, side))
+
+    send_first(0, has_right, n_left)
+    send_first(1, has_left, n_right)
+    for copy in small_in:
+        copy.wait()
     tile[...] = jnp.zeros_like(tile)
     row_base = quarter(resc[...])
     column_base = quarter(cesc[...])
@@ -95,57 +150,6 @@
     cb[me, 2:8, :] = jnp.broadcast_to(row_coef, (6, K))
     uall[me] = u[...]
 
-    for i in range(NP):
-        cols_in(i).wait()
-    pl.semaphore_wait(barrier, L - 1 + jnp.where(inner, 2, 1))
-
-    def layer_of(d):
-        return lax.rem(me + d, L)
-
-    def v_copy(src, c, i, side):
-        return remote(src, vline.at[c, i], vs.at[side, c], vr.at[c, i], "tensor",
-                      right if side == 0 else lft)
-
-    def x_copy(src, slot, dst):
-        return remote(src, vall.at[slot], xs, xr.at[slot], "layer", dst)
-
-    def u_copy(slot, dst):
-        return remote(u, uall.at[slot], us, ur.at[slot], "layer", dst)
-
-    def b_copy(slot, dst):
-        return remote(cb.at[me], cb.at[slot], bs, br.at[slot], "layer", dst)
-
-    def m_copy(slot, dst):
-        return remote(mout.at[dst], mi.at[slot], ms, mr, "layer", dst)
-
-    def l_copy(slot, dst):
-        return remote(lall.at[me], lall.at[slot], ls, lr.at[slot], "layer", dst)
-
-    def k_copy(src, side):
-        return remote(src, core_in.at[side], ks.at[side], kr.at[side], "tensor", right if side == 0 else lft)
-
-    def p_copy(src, d):
-        return remote(src, pin.at[d], ps, pr.at[d], "tensor", right)
-
-    def q_copy(src, d):
-        return remote(src, qin.at[d], qs, qr.at[d], "tensor", lft)
-
-    def send_own(i, side):
-        v_copy(vline.at[t, i], t, i, side).start()
-
-    def send_half(i, half, side):
-        rows = vline.at[t, i, pl.ds(half * (W // 2), W // 2)]
-        remote(rows, rows, vs.at[side, t], vr.at[t, i], "tensor", right if side == 0 else lft).start()
-
-    def send_first(side, onward, n):
-        @pl.when(onward)
-        def _():
-            loop(0, jnp.where(n > 0, 1, NP), lambda i: send_own(i, side))
-            pl.when((n > 0) & (NP > 1))(lambda: send_half(1, 0, side))
-
-    send_first(0, has_right, n_left)
-    send_first(1, has_left, n_right)
-
     def send_basis(d):
         dst = lax.rem(me - d + L, L)
         u_copy(me, dst).start()
@@ -300,8 +304,6 @@
         x = update(lf, guest_g[...], guest_u[...], pushed(final), guest_l[...])
         guest_x[...] = x.astype(BF16)
         guest_n[...] = lanes(x)
-        pl.when(t == T - 2)(lambda: p_copy(guest_x, final).start())
-        pl.when(t == 1)(lambda: q_copy(guest_x, final).start())
 
     blk = lax.rem(me, NP)
     home = lax.div(me, NP)
@@ -358,6 +360,8 @@
             device_id={"layer": lax.div(dst, T), "tensor": lax.rem(dst, T)}, device_id_type=MESH)
 
     loop(1, N, lambda d: n_copy(here, lax.rem(here + d, N)).start())
+    pl.when(t == T - 2)(lambda: p_copy(guest_x, final).start())
+    pl.when(t == 1)(lambda: q_copy(guest_x, final).start())
     nin[here] = tile[...]
 
     def sent(ref, sem, axis):
@@ -389,28 +393,26 @@
     tot = jnp.sum(nin[...], axis=0)
     fac = jnp.sqrt((tot[:, 0:L] + 1.0) / (tot[:, L:2 * L] + 1.0))
     factor[...] = jnp.broadcast_to(jnp.transpose(jnp.broadcast_to(fac, (8, L)))[:, 0:1], factor.shape)
-
     arrived.wait_send()
+
+    def scale(l, rows):
+        raw[l] = (rows.astype(F32) * factor[pl.ds(l, 1), 0:1]).astype(BF16)
+
+    def rescale(d):
+        l = layer_of(d)
+        scale(l, raw[l])
+
+    loop(0, jnp.where(inner, L, L - 1), rescale)
 
     @pl.when(t == T - 1)
     def _():
         p_copy(own.at[final], final).wait_recv()
-        raw[lf] = pin[final]
+        scale(lf, pin[final])
 
     @pl.when(t == 0)
     def _():
         q_copy(own.at[final], final).wait_recv()
-        raw[lf] = qin[final]
-
-
-def scale_kernel(raw, factor, out, buf, sem):
-    def one(l):
-        buf[l] = (raw[l].astype(F32) * factor[pl.ds(l, 1), 0:1]).astype(BF16)
-        pltpu.make_async_copy(buf.at[l], out.at[l], sem.at[l]).start()
-
-    L = raw.shape[0]
-    loop(0, L, one)
-    loop(0, L, lambda l: pltpu.make_async_copy(buf.at[l], out.at[l], sem.at[l]).wait())
+        scale(lf, qin[final])
 
 
 def solution(mesh):
@@ -425,13 +427,16 @@
         chunk = pltpu.VMEM((L, K, W), BF16)
         small = pltpu.VMEM((L, r, K), BF16)
         sem = pltpu.SemaphoreType.DMA
-        raw, factor = pl.pallas_call(
+        rows = pl.pallas_call(
             functools.partial(kernel, L, T, NP),
-            out_shape=(pltpu.VMEM((L, r, W), BF16), pltpu.VMEM((L, 128), F32)),
-            in_specs=[hbm, vmem, hbm, vmem, vmem, vmem, vmem],
-            out_specs=(vmem, vmem),
+            out_shape=pltpu.VMEM((L, r, W), BF16),
+            in_specs=[hbm] * 7,
+            out_specs=vmem,
             scratch_shapes=[
                 pltpu.VMEM((L, r, W), BF16),
+                pltpu.VMEM((r, K), BF16),
+                pltpu.VMEM((1, K), F32), pltpu.VMEM((1, K), F32),
+                pltpu.VMEM((1, 1), F32), pltpu.VMEM((1, 1), F32),
                 small,
                 pltpu.VMEM((L, W, K), BF16),
                 pltpu.VMEM((T, NP, Cr // NP, K), BF16),
@@ -451,6 +456,7 @@
                 pltpu.VMEM((2, L, 128), F32),
                 pltpu.VMEM((1, 128), F32),
                 pltpu.VMEM((L * T, 1, 128), F32),
+                pltpu.VMEM((L, 128), F32),
                 sem, sem((L,)),
                 sem, sem((L,)),
                 sem((2, T)), sem((T, NP)),
@@ -462,20 +468,13 @@
                 sem, sem((L,)),
                 sem, sem,
                 sem((3,)), sem((3,)),
-                sem, sem((NP,)),
+                sem, sem((NP,)), sem((5,)),
             ],
             compiler_params=pltpu.CompilerParams(
                 collective_id=0, has_side_effects=True, vmem_limit_bytes=67043328 - 2 * L * r * W - 256 * 1024),
         )(gradient, row_basis[0], column_basis[0], row_eigen, column_eigen,
           row_escape[:, None], column_escape[:, None])
-        return pl.pallas_call(
-            scale_kernel,
-            out_shape=jax.ShapeDtypeStruct((L, r, W), BF16),
-            in_specs=[vmem, vmem],
-            out_specs=hbm,
-            scratch_shapes=[pltpu.VMEM((L, r, W), BF16), sem((L,))],
-            compiler_params=pltpu.CompilerParams(vmem_limit_bytes=32 * 1024 * 1024),
-        )(raw, factor)
+        return rows
 
     in_specs = (
         P(None, "tensor", "layer"),

time: 175 us -> 171 us (0.977)
  Pallas kernels: 173 us -> 168 us
  local copies, waits for them, and re-layouts: 0 us -> 2.02 us
    pallas_call x2 -> x1, Pallas kernels: 173 us -> 168 us  [body(): pl.pallas_call(functools.partial(kernel, L, T, NP), out_shape=pltpu.VMEM(...]
    unnamed x0 -> x1, local copies, waits for them, and re-layouts: none -> 2.02 us
where the time goes in v5:
time: 171 us
  Pallas kernels  168 us (98%)
  local copies, waits for them, and re-layouts  2.02 us (1%)
    pallas_call x1, Pallas kernels, body(): pl.pallas_call(functools.partial(kernel, L, T, NP), out_shape=pltpu.VMEM(...  168 us

profile of v5, /device:TPU:0, one launch (start us, length us, event | category | flops | bytes accessed | tf_op | source)
XLA Modules:
  0.0 171.2 jit_solution(13011857821404922092)
XLA Ops:
  1.3 167.9 %shard_map.73 = bf16[8,256,1024]{2,1,0:T(8,128)(2,1)S(1)} custom-call(bf16[8,256,1024]{2,1,0:T(8,128)(2,1)} %g_hbm.1, bf16[256,256]{1,0:T(8,128)(2,1)} %bitcast.7, bf16[2048,256]{1,0:T(8,128)(2,1)} %bitcast.6, f32[1,256]{1,0:T(1,128)} %reig_hbm.1, f32[1,256]{1,0:T(1,128)} %ceig_hbm.1, f32[1,1]{1,0:T(1,128)} %bitcast.4.resc_hbm, f32[1,1]{1,0:T(1,128)} %bitcast.5.cesc_hbm), custom_call_target="tpu_custom_call" | custom-call | tf_op jit(solution)/shard_map/pallas_call | solution.py:430
  169.2 2.0 %copy.9 = bf16[8,256,1024]{2,1,0:T(8,128)(2,1)} copy(bf16[8,256,1024]{2,1,0:T(8,128)(2,1)S(1)} %shard_map.73) | data formatting | bytes 8388608

commit v6 on v5

--- a/solution.py
+++ b/solution.py
@@ -78,19 +78,32 @@
     for i in range(NP):
         cols_in(i).start()
 
+    bits = [1 << b for b in range(L.bit_length() - 1)]
+
+    def masks(k):
+        return [mask for mask in range(1, L) if bin(mask).count("1") == k]
+
+    def partner(mask):
+        index = me
+        for b in bits:
+            if mask & b:
+                index = index + b - 2 * b * lax.rem(lax.div(me, b), 2)
+        return index
+
     def greet(axis, index):
         pl.semaphore_signal(barrier, inc=1, device_id={axis: index}, device_id_type=MESH)
 
     barrier = pltpu.get_barrier_semaphore()
     pl.when(has_right)(lambda: greet("tensor", right))
     pl.when(has_left)(lambda: greet("tensor", lft))
-    loop(1, L, lambda d: greet("layer", lax.rem(me + d, L)))
+    for mask in masks(1):
+        greet("layer", partner(mask))
     for copy in small_in:
         copy.start()
     g_in.start()
     for i in range(NP):
         cols_in(i).wait()
-    pl.semaphore_wait(barrier, L - 1 + jnp.where(inner, 2, 1))
+    pl.semaphore_wait(barrier, len(bits) + jnp.where(inner, 2, 1))
 
     def layer_of(d):
         return lax.rem(me + d, L)
@@ -150,12 +163,17 @@
     cb[me, 2:8, :] = jnp.broadcast_to(row_coef, (6, K))
     uall[me] = u[...]
 
-    def send_basis(d):
-        dst = lax.rem(me - d + L, L)
+    def send_basis(mask):
+        dst = partner(mask)
         u_copy(me, dst).start()
         b_copy(me, dst).start()
 
-    loop(1, L, send_basis)
+    def take_basis(mask):
+        src = partner(mask)
+        u_copy(src, src).wait_recv()
+
+    for mask in masks(1):
+        send_basis(mask)
 
     def spread(c, i):
         dst = c * NP + i
@@ -178,7 +196,6 @@
 
         @pl.when(d > 0)
         def _():
-            u_copy(l, l).wait_recv()
             b_copy(l, l).wait_recv()
 
         block = g[l]
@@ -187,6 +204,11 @@
 
     g_in.wait()
     project(0)
+    for k in range(1, len(bits)):
+        for mask in masks(k):
+            take_basis(mask)
+        for mask in masks(k + 1):
+            send_basis(mask)
 
     def end_send(d):
         @pl.when((d >= 0) & (d < L))
@@ -319,6 +341,7 @@
         relay(s, n_right, 1, 1, has_left)
         pl.when(s == 1)(lambda: loop(0, NP, lambda i: spread(t, i)))
         pl.when(s < L)(lambda: end_send(s - 1))
+        pl.when(s == 1)(lambda: take_basis(L - 1))
         loop(jnp.clip(third * (s - 1) + 1, 1, L), jnp.clip(third * s + 1, 1, L), project)
         forward(s, t, p_copy, pin, 0)
         forward(s, T - 1 - t, q_copy, qin, 1)

time: 171 us -> 170 us (level)
  Pallas kernels: 168 us -> 166 us
where the time goes in v6:
time: 170 us
  Pallas kernels  166 us (98%)
  local copies, waits for them, and re-layouts  2.02 us (1%)
    pallas_call x1, Pallas kernels, body(): pl.pallas_call(functools.partial(kernel, L, T, NP), out_shape=pltpu.VMEM(...  166 us

profile of v6, /device:TPU:0, one launch (start us, length us, event | category | flops | bytes accessed | tf_op | source)
XLA Modules:
  0.0 169.8 jit_solution(11353411598657414483)
XLA Ops:
  1.3 166.4 %shard_map.73 = bf16[8,256,1024]{2,1,0:T(8,128)(2,1)S(1)} custom-call(bf16[8,256,1024]{2,1,0:T(8,128)(2,1)} %g_hbm.1, bf16[256,256]{1,0:T(8,128)(2,1)} %bitcast.7, bf16[2048,256]{1,0:T(8,128)(2,1)} %bitcast.6, f32[1,256]{1,0:T(1,128)} %reig_hbm.1, f32[1,256]{1,0:T(1,128)} %ceig_hbm.1, f32[1,1]{1,0:T(1,128)} %bitcast.4.resc_hbm, f32[1,1]{1,0:T(1,128)} %bitcast.5.cesc_hbm), custom_call_target="tpu_custom_call" | custom-call | tf_op jit(solution)/shard_map/pallas_call | solution.py:453
  167.7 2.0 %copy.9 = bf16[8,256,1024]{2,1,0:T(8,128)(2,1)} copy(bf16[8,256,1024]{2,1,0:T(8,128)(2,1)S(1)} %shard_map.73) | data formatting | bytes 8388608

commit v7 on v6

--- a/solution.py
+++ b/solution.py
@@ -51,9 +51,9 @@
     L, T, NP,
     g_hbm, u_hbm, cols_hbm, reig_hbm, ceig_hbm, resc_hbm, cesc_hbm,
     raw,
-    g, u, reig, ceig, resc, cesc, uall, vall, vline, own, pin, qin, mout, mi, mid, lall, core_out, core_in, core_sum, cb,
+    g, u, reig, ceig, resc, cesc, uall, vall, vline, own, pin, qin, mout, mpal, mi, mid, lall, core_out, core_in, core_sum, cb,
     guest_g, guest_u, guest_l, guest_x, guest_n, nsend, tile, nin, factor,
-    us, ur, bs, br, vs, vr, xs, xr, ms, mr, ks, kr, ls, lr, ps, pr, qs, qr, ns, nr, hs, hr, gs, cs, es,
+    us, ur, bs, br, vs, vr, xs, xr, ms, mr, ks, kr, ls, lr, ps, pr, qs, qr, ns, nr, hs, hr, zs, zr, gs, cs, es,
 ):
     me = lax.axis_index("layer")
     t = lax.axis_index("tensor")
@@ -251,27 +251,42 @@
     def middle(d):
         l = layer_of(d)
         pl.when(d > 0)(lambda: x_copy(vall.at[l], l, l).wait_recv())
-        m = dot(g[l], vall[l]).astype(BF16)
-
-        @pl.when(d == 0)
-        def _():
-            mi[me] = m
-
-        @pl.when(d > 0)
-        def _():
-            mout[l] = m
-            m_copy(me, l).start()
+        mout[l] = dot(g[l], vall[l]).astype(BF16)
+        pl.when(lax.rem(l, 2) != lax.rem(me, 2))(lambda: z_copy(l).start())
+
+    def z_copy(l):
+        pal = me + 1 - 2 * lax.rem(me, 2)
+        return remote(mout.at[l], mpal.at[lax.div(l, 2)], zs, zr, "layer", pal)
+
+    half = L // 2
+
+    def add_pairs():
+        remote(mpal, mpal, zs, zr, "layer", me).wait_recv()
+
+        def one(j):
+            l = lax.rem(me, 2) + 2 * j
+            both = (mout[l].astype(F32) + mpal[j].astype(F32)).astype(BF16)
+
+            @pl.when(l == me)
+            def _():
+                mi[j] = both
+
+            @pl.when(l != me)
+            def _():
+                mout[l] = both
+                m_copy(lax.div(me, 2), l).start()
+
+        loop(0, half, one)
 
     def gather_middle():
-        total = mi[me].astype(F32)
-        mid[...] = total
-
-        remote(mout.at[pl.ds(0, L - 1)], mi.at[pl.ds(0, L - 1)], ms, mr, "layer", me).wait_recv()
-
-        def add(d):
-            mid[...] += mi[layer_of(d)].astype(F32)
-
-        loop(1, L, add)
+        add_pairs()
+        remote(mout.at[pl.ds(0, half - 1)], mi.at[pl.ds(0, half - 1)], ms, mr, "layer", me).wait_recv()
+        mid[...] = mi[0].astype(F32)
+
+        def add(j):
+            mid[...] += mi[j].astype(F32)
+
+        loop(1, half, add)
         core_out[...] = dot(u[...], mid[...].astype(BF16), ((0,), (0,))).astype(BF16)
 
         @pl.when(t == 0)
@@ -391,8 +406,10 @@
         remote(ref, ref, sem, sem, axis, 0).wait_send()
 
     most = pl.ds(0, L - 1)
-    for ref, sem in ((uall, us), (cb, bs), (vall, xs), (mout, ms), (lall, ls)):
+    for ref, sem in ((uall, us), (cb, bs), (vall, xs), (lall, ls)):
         sent(ref.at[most], sem, "layer")
+    sent(mout.at[pl.ds(0, half - 1)], ms, "layer")
+    sent(mpal, zs, "layer")
     pl.when(has_right)(lambda: k_copy(core_out, 0).wait_send())
     pl.when(has_left)(lambda: k_copy(core_out, 1).wait_send())
 
@@ -464,7 +481,9 @@
                 pltpu.VMEM((L, W, K), BF16),
                 pltpu.VMEM((T, NP, Cr // NP, K), BF16),
                 chunk, chunk, chunk,
-                small, small,
+                small,
+                pltpu.VMEM((L // 2, r, K), BF16),
+                pltpu.VMEM((L // 2, r, K), BF16),
                 pltpu.VMEM((r, K), F32),
                 small,
                 pltpu.VMEM((K, K), BF16),
@@ -491,6 +510,7 @@
                 sem, sem((L,)),
                 sem, sem,
                 sem((3,)), sem((3,)),
+                sem, sem,
                 sem, sem((NP,)), sem((5,)),
             ],
             compiler_params=pltpu.CompilerParams(

time: 170 us -> 170 us (level)
  no operation moved by 1% of the time
where the time goes in v7:
time: 170 us
  Pallas kernels  166 us (98%)
  local copies, waits for them, and re-layouts  2.02 us (1%)
    pallas_call x1, Pallas kernels, body(): pl.pallas_call(functools.partial(kernel, L, T, NP), out_shape=pltpu.VMEM(...  166 us

profile of v7, /device:TPU:0, one launch (start us, length us, event | category | flops | bytes accessed | tf_op | source)
XLA Modules:
  0.0 169.8 jit_solution(7221568619549987588)
XLA Ops:
  1.3 166.5 %shard_map.73 = bf16[8,256,1024]{2,1,0:T(8,128)(2,1)S(1)} custom-call(bf16[8,256,1024]{2,1,0:T(8,128)(2,1)} %g_hbm.1, bf16[256,256]{1,0:T(8,128)(2,1)} %bitcast.7, bf16[2048,256]{1,0:T(8,128)(2,1)} %bitcast.6, f32[1,256]{1,0:T(1,128)} %reig_hbm.1, f32[1,256]{1,0:T(1,128)} %ceig_hbm.1, f32[1,1]{1,0:T(1,128)} %bitcast.4.resc_hbm, f32[1,1]{1,0:T(1,128)} %bitcast.5.cesc_hbm), custom_call_target="tpu_custom_call" | custom-call | tf_op jit(solution)/shard_map/pallas_call | solution.py:470
  167.8 2.0 %copy.9 = bf16[8,256,1024]{2,1,0:T(8,128)(2,1)} copy(bf16[8,256,1024]{2,1,0:T(8,128)(2,1)S(1)} %shard_map.73) | data formatting | bytes 8388608

commit v8 on v7

--- a/solution.py
+++ b/solution.py
@@ -101,8 +101,7 @@
     for copy in small_in:
         copy.start()
     g_in.start()
-    for i in range(NP):
-        cols_in(i).wait()
+    cols_in(0).wait()
     pl.semaphore_wait(barrier, len(bits) + jnp.where(inner, 2, 1))
 
     def layer_of(d):
@@ -146,9 +145,13 @@
     def send_first(side, onward, n):
         @pl.when(onward)
         def _():
-            loop(0, jnp.where(n > 0, 1, NP), lambda i: send_own(i, side))
+            loop(1, jnp.where(n > 0, 1, NP), lambda i: send_own(i, side))
             pl.when((n > 0) & (NP > 1))(lambda: send_half(1, 0, side))
 
+    pl.when(has_right)(lambda: send_own(0, 0))
+    pl.when(has_left)(lambda: send_own(0, 1))
+    for i in range(1, NP):
+        cols_in(i).wait()
     send_first(0, has_right, n_left)
     send_first(1, has_left, n_right)
     for copy in small_in:

time: 170 us -> 170 us (level)
  no operation moved by 1% of the time
where the time goes in v8:
time: 170 us
  Pallas kernels  166 us (98%)
  local copies, waits for them, and re-layouts  2.02 us (1%)
    pallas_call x1, Pallas kernels, body(): pl.pallas_call(functools.partial(kernel, L, T, NP), out_shape=pltpu.VMEM(...  166 us

profile of v8, /device:TPU:0, one launch (start us, length us, event | category | flops | bytes accessed | tf_op | source)
XLA Modules:
  0.0 169.8 jit_solution(16837939432111586471)
XLA Ops:
  1.3 166.5 %shard_map.73 = bf16[8,256,1024]{2,1,0:T(8,128)(2,1)S(1)} custom-call(bf16[8,256,1024]{2,1,0:T(8,128)(2,1)} %g_hbm.1, bf16[256,256]{1,0:T(8,128)(2,1)} %bitcast.7, bf16[2048,256]{1,0:T(8,128)(2,1)} %bitcast.6, f32[1,256]{1,0:T(1,128)} %reig_hbm.1, f32[1,256]{1,0:T(1,128)} %ceig_hbm.1, f32[1,1]{1,0:T(1,128)} %bitcast.4.resc_hbm, f32[1,1]{1,0:T(1,128)} %bitcast.5.cesc_hbm), custom_call_target="tpu_custom_call" | custom-call | tf_op jit(solution)/shard_map/pallas_call | solution.py:473
  167.8 2.0 %copy.9 = bf16[8,256,1024]{2,1,0:T(8,128)(2,1)} copy(bf16[8,256,1024]{2,1,0:T(8,128)(2,1)S(1)} %shard_map.73) | data formatting | bytes 8388608
